TPU v7x, 8 devices: a whole 2x2x1 slice. The times are simulated.
8 devices in a mesh: fsdp: 8 (over z, y, x, core).
Axes of the slice: x: 2, y: 2, z: 1, core: 2. Of those that a mesh axis runs over, the one named last changes fastest.
Arguments:
- w_query: float32 [2, 576, 576], P(None, 'fsdp')
- w_key: float32 [2, 576, 192], P(None, 'fsdp')
- w_value: float32 [2, 576, 192], P(None, 'fsdp')
- w_out: float32 [2, 576, 576], P(None, 'fsdp')
- w_gate: float32 [2, 576, 1536], P(None, 'fsdp')
- w_up: float32 [2, 576, 1536], P(None, 'fsdp')
- w_down: float32 [2, 1536, 576], P(None, 'fsdp')
- gain_attn: float32 [2, 576], P(None, 'fsdp')
- gain_mlp: float32 [2, 576], P(None, 'fsdp')
- rope_cos: float32 [256, 32], replicated
- rope_sin: float32 [256, 32], replicated
- x_in: bfloat16 [32, 256, 576], P('fsdp')
- y_cot: bfloat16 [32, 256, 576], P('fsdp')
Outputs:
- output 1: bfloat16 [32, 256, 576], P('fsdp')
- output 2: bfloat16 [32, 256, 576], P('fsdp')
- output 3: float32 [2, 576, 576], P(None, 'fsdp')
- output 4: float32 [2, 576, 192], P(None, 'fsdp')
- output 5: float32 [2, 576, 192], P(None, 'fsdp')
- output 6: float32 [2, 576, 576], P(None, 'fsdp')
- output 7: float32 [2, 576, 1536], P(None, 'fsdp')
- output 8: float32 [2, 576, 1536], P(None, 'fsdp')
- output 9: float32 [2, 1536, 576], P(None, 'fsdp')
- output 10: float32 [2, 576], P(None, 'fsdp')
- output 11: float32 [2, 576], P(None, 'fsdp')
All inputs are finite; a program needn't handle non-finite values.
Results may differ from a plain program's by a relative error of at most 0.02.
Values are sent between devices in bfloat16 or wider.
A program may use at most 1 GiB of HBM per device.

v0:
```python
import jax
import jax.numpy as jnp
from jax import lax
from jax.sharding import PartitionSpec as P

NORM_EPS = 1e-5
MASK_VALUE = -1e30


def rms_forward(values, gain):
    vals32 = values.astype(jnp.float32)
    inv_rms = lax.rsqrt(jnp.mean(vals32 * vals32, axis=-1, keepdims=True) + NORM_EPS)
    normed = (vals32 * inv_rms * gain.astype(jnp.float32)).astype(jnp.bfloat16)
    return normed, inv_rms


def rms_backward(values, inv_rms, gain, grad_normed):
    scaled = values.astype(jnp.float32) * inv_rms
    grad_scaled = grad_normed * gain.astype(jnp.float32)
    grad_gain = jnp.sum(grad_normed * scaled, axis=(0, 1))
    grad_values = inv_rms * (grad_scaled - scaled * jnp.mean(grad_scaled * scaled, axis=-1, keepdims=True))
    return grad_values, grad_gain


def rotary(heads32, rope_cos, rope_sin, sin_sign):
    half_dim = rope_cos.shape[-1]
    first_half = heads32[..., :half_dim]
    second_half = heads32[..., half_dim:]
    cos_b = rope_cos[None, :, None, :]
    sin_b = sin_sign * rope_sin[None, :, None, :]
    return jnp.concatenate([first_half * cos_b - second_half * sin_b, second_half * cos_b + first_half * sin_b], axis=-1)


def layer_forward(weights, rope_cos, rope_sin, hidden):
    w_query, w_key, w_value, w_out, w_gate, w_up, w_down, gain_attn, gain_mlp = weights
    batch_size = hidden.shape[0]
    seq_len = hidden.shape[1]
    head_dim = 2 * rope_cos.shape[-1]
    kv_heads = w_key.shape[1] // head_dim
    num_heads = w_query.shape[1] // head_dim
    group_size = num_heads // kv_heads
    normed, inv_rms_attn = rms_forward(hidden, gain_attn)
    q_proj = jnp.einsum("bsd,df->bsf", normed, w_query, preferred_element_type=jnp.float32)
    q_heads = rotary(q_proj.reshape(batch_size, seq_len, num_heads, head_dim), rope_cos, rope_sin, 1.0)
    q_heads = q_heads.astype(jnp.bfloat16).reshape(batch_size, seq_len, kv_heads, group_size, head_dim)
    k_proj = jnp.einsum("bsd,df->bsf", normed, w_key, preferred_element_type=jnp.float32)
    k_heads = rotary(k_proj.reshape(batch_size, seq_len, kv_heads, head_dim), rope_cos, rope_sin, 1.0).astype(jnp.bfloat16)
    v_heads = jnp.einsum("bsd,df->bsf", normed, w_value, preferred_element_type=jnp.float32)
    v_heads = v_heads.astype(jnp.bfloat16).reshape(batch_size, seq_len, kv_heads, head_dim)
    scores = jnp.einsum("bqkgd,bskd->bkgqs", q_heads, k_heads, preferred_element_type=jnp.float32) * head_dim ** -0.5
    positions = jnp.arange(seq_len)
    scores = jnp.where(positions[:, None] >= positions[None, :], scores, MASK_VALUE)
    attn_probs = jax.nn.softmax(scores, axis=-1).astype(jnp.bfloat16)
    attn_heads = jnp.einsum("bkgqs,bskd->bqkgd", attn_probs, v_heads, preferred_element_type=jnp.float32)
    attn_heads = attn_heads.astype(jnp.bfloat16).reshape(batch_size, seq_len, num_heads * head_dim)
    attn_proj = jnp.einsum("bsf,fd->bsd", attn_heads, w_out, preferred_element_type=jnp.float32)
    mid_hidden = (hidden.astype(jnp.float32) + attn_proj).astype(jnp.bfloat16)
    normed_mlp, inv_rms_mlp = rms_forward(mid_hidden, gain_mlp)
    gate_pre = jnp.einsum("bsd,df->bsf", normed_mlp, w_gate, preferred_element_type=jnp.float32)
    up_proj = jnp.einsum("bsd,df->bsf", normed_mlp, w_up, preferred_element_type=jnp.float32)
    mlp_act = (jax.nn.silu(gate_pre) * up_proj).astype(jnp.bfloat16)
    down_proj = jnp.einsum("bsf,fd->bsd", mlp_act, w_down, preferred_element_type=jnp.float32)
    out_hidden = (mid_hidden.astype(jnp.float32) + down_proj).astype(jnp.bfloat16)
    saved_acts = (hidden, inv_rms_attn, normed, q_heads, k_heads, v_heads, attn_probs, attn_heads, mid_hidden, inv_rms_mlp, normed_mlp, gate_pre, up_proj, mlp_act)
    return out_hidden, saved_acts


def layer_backward(weights, rope_cos, rope_sin, saved_acts, grad_out):
    w_query, w_key, w_value, w_out, w_gate, w_up, w_down, gain_attn, gain_mlp = weights
    (hidden, inv_rms_attn, normed, q_heads, k_heads, v_heads, attn_probs, attn_heads, mid_hidden, inv_rms_mlp, normed_mlp, gate_pre, up_proj, mlp_act) = saved_acts
    batch_size = hidden.shape[0]
    seq_len = hidden.shape[1]
    head_dim = 2 * rope_cos.shape[-1]
    kv_heads = k_heads.shape[2]
    num_heads = kv_heads * q_heads.shape[3]
    grad_w_down = jnp.einsum("bsf,bsd->fd", mlp_act, grad_out, preferred_element_type=jnp.float32)
    grad_act = jnp.einsum("bsd,fd->bsf", grad_out, w_down, preferred_element_type=jnp.float32)
    gate_sig = jax.nn.sigmoid(gate_pre)
    grad_up = (grad_act * gate_pre * gate_sig).astype(jnp.bfloat16)
    grad_gate = (grad_act * up_proj * gate_sig * (1.0 + gate_pre * (1.0 - gate_sig))).astype(jnp.bfloat16)
    grad_w_gate = jnp.einsum("bsd,bsf->df", normed_mlp, grad_gate, preferred_element_type=jnp.float32)
    grad_w_up = jnp.einsum("bsd,bsf->df", normed_mlp, grad_up, preferred_element_type=jnp.float32)
    grad_normed_mlp = (jnp.einsum("bsf,df->bsd", grad_gate, w_gate, preferred_element_type=jnp.float32)
                       + jnp.einsum("bsf,df->bsd", grad_up, w_up, preferred_element_type=jnp.float32))
    grad_mid_norm, grad_gain_mlp = rms_backward(mid_hidden, inv_rms_mlp, gain_mlp, grad_normed_mlp)
    grad_mid = grad_out.astype(jnp.float32) + grad_mid_norm
    grad_mid_bf = grad_mid.astype(jnp.bfloat16)
    grad_w_out = jnp.einsum("bsf,bsd->fd", attn_heads, grad_mid_bf, preferred_element_type=jnp.float32)
    grad_attn = jnp.einsum("bsd,fd->bsf", grad_mid_bf, w_out, preferred_element_type=jnp.float32)
    grad_attn = grad_attn.astype(jnp.bfloat16).reshape(batch_size, seq_len, kv_heads, -1, head_dim)
    grad_v = jnp.einsum("bkgqs,bqkgd->bskd", attn_probs, grad_attn, preferred_element_type=jnp.float32)
    grad_v = grad_v.astype(jnp.bfloat16).reshape(batch_size, seq_len, -1)
    grad_probs = jnp.einsum("bqkgd,bskd->bkgqs", grad_attn, v_heads, preferred_element_type=jnp.float32)
    probs32 = attn_probs.astype(jnp.float32)
    grad_scores = probs32 * (grad_probs - jnp.sum(probs32 * grad_probs, axis=-1, keepdims=True)) * head_dim ** -0.5
    grad_scores = grad_scores.astype(jnp.bfloat16)
    grad_q = jnp.einsum("bkgqs,bskd->bqkgd", grad_scores, k_heads, preferred_element_type=jnp.float32)
    grad_q = rotary(grad_q.reshape(batch_size, seq_len, num_heads, head_dim), rope_cos, rope_sin, -1.0)
    grad_q = grad_q.astype(jnp.bfloat16).reshape(batch_size, seq_len, -1)
    grad_k = jnp.einsum("bkgqs,bqkgd->bskd", grad_scores, q_heads, preferred_element_type=jnp.float32)
    grad_k = rotary(grad_k, rope_cos, rope_sin, -1.0).astype(jnp.bfloat16).reshape(batch_size, seq_len, -1)
    grad_w_query = jnp.einsum("bsd,bsf->df", normed, grad_q, preferred_element_type=jnp.float32)
    grad_w_key = jnp.einsum("bsd,bsf->df", normed, grad_k, preferred_element_type=jnp.float32)
    grad_w_value = jnp.einsum("bsd,bsf->df", normed, grad_v, preferred_element_type=jnp.float32)
    grad_normed = (jnp.einsum("bsf,df->bsd", grad_q, w_query, preferred_element_type=jnp.float32)
                   + jnp.einsum("bsf,df->bsd", grad_k, w_key, preferred_element_type=jnp.float32)
                   + jnp.einsum("bsf,df->bsd", grad_v, w_value, preferred_element_type=jnp.float32))
    grad_hidden_norm, grad_gain_attn = rms_backward(hidden, inv_rms_attn, gain_attn, grad_normed)
    grad_hidden = (grad_mid + grad_hidden_norm).astype(jnp.bfloat16)
    layer_grads = (grad_w_query, grad_w_key, grad_w_value, grad_w_out, grad_w_gate, grad_w_up, grad_w_down, grad_gain_attn, grad_gain_mlp)
    return grad_hidden, layer_grads


def solution(mesh):
    shard_spec = P(None, "fsdp")
    batch_spec = P("fsdp")

    def gather_layer(masters, layer_idx):
        return tuple(lax.all_gather(master[layer_idx].astype(jnp.bfloat16), "fsdp", axis=0, tiled=True) for master in masters)

    def local_step(w_query, w_key, w_value, w_out, w_gate, w_up, w_down, gain_attn, gain_mlp, rope_cos, rope_sin, x_in, y_cot):
        masters = (w_query, w_key, w_value, w_out, w_gate, w_up, w_down, gain_attn, gain_mlp)
        num_layers = w_query.shape[0]
        hidden = x_in
        saved_layers = []
        for layer_idx in range(num_layers):
            weights = gather_layer(masters, layer_idx)
            hidden, saved_acts = layer_forward(weights, rope_cos, rope_sin, hidden)
            saved_layers.append(saved_acts)
        masters, saved_layers, hidden = lax.optimization_barrier((masters, saved_layers, hidden))
        grad_hidden = y_cot
        grad_layers = []
        for layer_idx in reversed(range(num_layers)):
            weights = gather_layer(masters, layer_idx)
            grad_hidden, layer_grads = layer_backward(weights, rope_cos, rope_sin, saved_layers[layer_idx], grad_hidden)
            grad_layers.insert(0, tuple(lax.psum_scatter(grad_full, "fsdp", scatter_dimension=0, tiled=True) for grad_full in layer_grads))
        grad_stacked = tuple(jnp.stack([layer_part[tensor_idx] for layer_part in grad_layers]) for tensor_idx in range(len(masters)))
        return (hidden, grad_hidden) + grad_stacked

    in_specs = (shard_spec,) * 9 + (P(), P(), batch_spec, batch_spec)
    out_specs = (batch_spec, batch_spec) + (shard_spec,) * 9
    return jax.shard_map(local_step, mesh=mesh, in_specs=in_specs, out_specs=out_specs, check_vma=False)
```

profile of v0, /device:TPU:0, one launch (start us, length us, event | category | flops | bytes accessed | tf_op | source)
XLA Modules:
  0.0 971.3 jit_solution(2598664112538925281)
XLA Ops:
  15.6 25.3 %all-reduce.18 = (bf16[576]{0:T(1024)(128)(2,1)S(1)}, bf16[576]{0:T(1024)(128)(2,1)S(1)}, bf16[576]{0:T(1024)(128)(2,1)S(1)}, bf16[576]{0:T(1024)(128)(2,1)S(1)}) all-reduce(bf16[576]{0:T(1024)(128)(2,1)S(1)} %dynamic-update-slice, bf16[576]{0:T(1024)(128)(2,1)S(1)} %dynamic-update-slice.1, ...), channel_id=2, replica_groups=mesh['fsdp'=8] {'fsdp'}, use_global_device_ids=true, to_apply=%add | all-reduce | flops 2304 | bytes 9216
  41.0 17.7 %all-gather.1 = bf16[1,576,576]{2,1,0:T(8,128)(2,1)S(1)} all-gather(bf16[1,72,576]{2,1,0:T(8,128)(2,1)S(1)} %get-tuple-element.146), channel_id=3, replica_groups=mesh['fsdp'=8] {'fsdp'}, dimensions={1}, use_global_device_ids=true | all-gather | bytes 746496 | tf_op jit(solution)/shard_map/all_gather | solution.py:119
  58.7 12.4 %all-gather.2 = bf16[1,576,192]{2,1,0:T(8,128)(2,1)S(1)} all-gather(bf16[1,72,192]{2,1,0:T(8,128)(2,1)S(1)} %get-tuple-element.154), channel_id=4, replica_groups=mesh['fsdp'=8] {'fsdp'}, dimensions={1}, use_global_device_ids=true | all-gather | bytes 248832 | tf_op jit(solution)/shard_map/all_gather | solution.py:119
  74.8 12.1 %all-gather.3 = bf16[1,576,192]{2,1,0:T(8,128)(2,1)S(1)} all-gather(bf16[1,72,192]{2,1,0:T(8,128)(2,1)S(1)} %get-tuple-element.152), channel_id=5, replica_groups=mesh['fsdp'=8] {'fsdp'}, dimensions={1}, use_global_device_ids=true | all-gather | bytes 248832 | tf_op jit(solution)/shard_map/all_gather | solution.py:119
  89.4 8.6 fusion.163
  99.0 13.9 %all-gather.4 = bf16[1,576,576]{2,1,0:T(8,128)(2,1)S(1)} all-gather(bf16[1,72,576]{2,1,0:T(8,128)(2,1)S(1)} %get-tuple-element.144), channel_id=6, replica_groups=mesh['fsdp'=8] {'fsdp'}, dimensions={1}, use_global_device_ids=true | all-gather | bytes 746496 | tf_op jit(solution)/shard_map/all_gather | solution.py:119
  112.9 4.9 divide_convert_fusion.1
  121.8 14.7 %all-gather.10 = bf16[1,576,576]{2,1,0:T(8,128)(2,1)} all-gather(bf16[1,72,576]{2,1,0:T(8,128)(2,1)S(1)} %get-tuple-element.145), channel_id=12, replica_groups=mesh['fsdp'=8] {'fsdp'}, dimensions={1}, use_global_device_ids=true | all-gather | bytes 746496 | tf_op jit(solution)/shard_map/all_gather | solution.py:119
  136.5 12.2 %all-gather.11 = bf16[1,576,192]{2,1,0:T(8,128)(2,1)S(1)} all-gather(bf16[1,72,192]{2,1,0:T(8,128)(2,1)S(1)} %get-tuple-element.153), channel_id=13, replica_groups=mesh['fsdp'=8] {'fsdp'}, dimensions={1}, use_global_device_ids=true | all-gather | bytes 248832 | tf_op jit(solution)/shard_map/all_gather | solution.py:119
  148.7 12.1 %all-gather.12 = bf16[1,576,192]{2,1,0:T(8,128)(2,1)} all-gather(bf16[1,72,192]{2,1,0:T(8,128)(2,1)S(1)} %copy-done.63), channel_id=14, replica_groups=mesh['fsdp'=8] {'fsdp'}, dimensions={1}, use_global_device_ids=true | all-gather | bytes 248832 | tf_op jit(solution)/shard_map/all_gather | solution.py:119
  160.8 13.2 %all-gather.13 = bf16[1,576,576]{2,1,0:T(8,128)(2,1)} all-gather(bf16[1,72,576]{2,1,0:T(8,128)(2,1)S(1)} %get-tuple-element.143), channel_id=15, replica_groups=mesh['fsdp'=8] {'fsdp'}, dimensions={1}, use_global_device_ids=true | all-gather | bytes 746496 | tf_op jit(solution)/shard_map/all_gather | solution.py:119
  175.3 6.3 fusion.65
  181.7 10.7 %multiply_convert_fusion.3 = (bf16[4,256,1536]{2,1,0:T(8,128)(2,1)}, f32[4,256,1536]{2,1,0:T(8,128)}) fusion(f32[4,256,1536]{2,1,0:T(8,128)} %fusion.65, bf16[4,256,576]{1,2,0:T(8,128)(2,1)} %copy-done.37, bf16[1,576,1536]{2,1,0:T(8,128)(2,1)} %all-gather.51.cloned.1.call-done), kind=kOutput, calls=%fused_computation.36 | convolution fusion | flops 1821376512 | bytes 18677760 | tf_op jit(solution)/shard_map/bsd,df->bsf/dot_general | solution.py:60
  192.4 4.7 fusion.35
  203.2 8.0 fusion.168
  211.2 4.9 divide_convert_fusion
  217.0 12.0 %convolution_convert_fusion = bf16[4,3,64,3,256]{4,2,3,1,0:T(8,128)(2,1)S(1)} fusion(bf16[4,256,3,64,1]{1,3,4,2,0:T(8,128)(2,1)S(1)} %bitcast.507, bf16[4,3,3,256,256]{3,4,2,1,0:T(8,128)(2,1)S(1)} %divide_convert_fusion), kind=kOutput, calls=%fused_computation.125 | convolution fusion | flops 302579712 | bytes 6291456 | tf_op jit(solution)/shard_map/bkgqs,bskd->bqkgd/dot_general | solution.py:54
  232.7 7.1 fusion.61
  239.8 10.6 %multiply_convert_fusion.2 = (bf16[4,256,1536]{2,1,0:T(8,128)(2,1)}, f32[4,256,1536]{2,1,0:T(8,128)}) fusion(f32[4,256,1536]{2,1,0:T(8,128)} %fusion.61, bf16[4,256,576]{1,2,0:T(8,128)(2,1)} %fusion.41, bf16[1,576,1536]{2,1,0:T(8,128)(2,1)} %all-gather.57.cloned.1.call-done), kind=kOutput, calls=%fused_computation.35 | convolution fusion | flops 1821376512 | bytes 18677760 | tf_op jit(solution)/shard_map/bsd,df->bsf/dot_general | solution.py:60
  250.4 5.9 fusion.42
  263.8 22.4 %all-reduce.17 = (bf16[576]{0:T(1024)(128)(2,1)S(1)}, bf16[576]{0:T(1024)(128)(2,1)S(1)}, bf16[576]{0:T(1024)(128)(2,1)S(1)}, bf16[576]{0:T(1024)(128)(2,1)S(1)}) all-reduce(bf16[576]{0:T(1024)(128)(2,1)S(1)} %dynamic-update-slice.4, bf16[576]{0:T(1024)(128)(2,1)S(1)} %dynamic-update-slice.5, ...), channel_id=23, replica_groups=mesh['fsdp'=8] {'fsdp'}, use_global_device_ids=true, to_apply=%add.4 | all-reduce | flops 2304 | bytes 9216
  288.9 13.2 %all-gather.25 = bf16[1,576,192]{2,1,0:T(8,128)(2,1)} all-gather(bf16[1,72,192]{2,1,0:T(8,128)(2,1)S(1)} %get-tuple-element.148), channel_id=27, replica_groups=mesh['fsdp'=8] {'fsdp'}, dimensions={1}, use_global_device_ids=true | all-gather | bytes 248832 | tf_op jit(solution)/shard_map/all_gather | solution.py:119
  302.7 12.5 %all-gather.24 = bf16[1,576,192]{2,1,0:T(8,128)(2,1)} all-gather(bf16[1,72,192]{2,1,0:T(8,128)(2,1)S(1)} %get-tuple-element.150), channel_id=26, replica_groups=mesh['fsdp'=8] {'fsdp'}, dimensions={1}, use_global_device_ids=true | all-gather | bytes 248832 | tf_op jit(solution)/shard_map/all_gather | solution.py:119
  315.3 15.1 %all-gather.22 = bf16[1,576,576]{2,1,0:T(8,128)(2,1)} all-gather(bf16[1,72,576]{2,1,0:T(8,128)(2,1)S(1)} %get-tuple-element.142), channel_id=24, replica_groups=mesh['fsdp'=8] {'fsdp'}, dimensions={1}, use_global_device_ids=true | all-gather | bytes 746496 | tf_op jit(solution)/shard_map/all_gather | solution.py:119
  331.0 14.4 %all-gather.23 = bf16[1,576,576]{2,1,0:T(8,128)(2,1)} all-gather(bf16[1,72,576]{2,1,0:T(8,128)(2,1)S(1)} %get-tuple-element.140), channel_id=25, replica_groups=mesh['fsdp'=8] {'fsdp'}, dimensions={1}, use_global_device_ids=true | all-gather | bytes 746496 | tf_op jit(solution)/shard_map/all_gather | solution.py:119
  345.4 13.6 %all-gather.31 = bf16[1,576,576]{2,1,0:T(8,128)(2,1)} all-gather(bf16[1,72,576]{2,1,0:T(8,128)(2,1)S(1)} %get-tuple-element.141), channel_id=33, replica_groups=mesh['fsdp'=8] {'fsdp'}, dimensions={1}, use_global_device_ids=true | all-gather | bytes 746496 | tf_op jit(solution)/shard_map/all_gather | solution.py:119
  359.1 10.9 %fusion.14 = (bf16[4,256,1536]{2,1,0:T(8,128)(2,1)}, bf16[4,256,1536]{2,1,0:T(8,128)(2,1)}) fusion(f32[4,256,1536]{2,1,0:T(8,128)} %get-tuple-element.52, f32[4,256,1536]{2,1,0:T(8,128)} %fusion.61, bf16[4,256,576]{1,2,0:T(8,128)(2,1)} %param.25, bf16[1,1536,576]{2,1,0:T(8,128)(2,1)} %all-gather.61.cloned.1.call-done), kind=kOutput, calls=%fused_computation.28 | convolution fusion | flops 1832386560 | bytes 21823488 | tf_op jit(solution)/shard_map/bsd,fd->bsf/dot_general | solution.py:77
  370.1 6.0 fusion.55
  376.1 6.6 multiply_reduce_fusion
  384.7 2.8 convolution_convert_fusion.3
  389.1 5.1 fusion.104
  394.2 14.0 %fusion.20 = f32[4,3,64,3,256]{4,2,3,1,0:T(8,128)} fusion(bf16[4,3,3,256,256]{3,4,2,1,0:T(8,128)(2,1)} %copy-done.1, f32[4,3,256,256,3]{3,2,4,1,0:T(8,128)} %fusion.104, bf16[4,256,3,64]{1,3,2,0:T(8,128)(2,1)S(1)} %copy-done.59), kind=kOutput, calls=%fused_computation.40 | convolution fusion | flops 318514432 | bytes 16908288 | tf_op jit(solution)/shard_map/bkgqs,bskd->bqkgd/dot_general | solution.py:97
  408.2 13.8 %fusion.77 = f32[4,256,3,64]{1,3,2,0:T(8,128)} fusion(bf16[4,256,3,3,64]{1,4,3,2,0:T(8,128)(2,1)} %pad_maximum_fusion.1, bf16[4,3,3,256,256]{3,4,2,1,0:T(8,128)(2,1)} %copy-done.1, f32[4,3,256,256,3]{3,2,4,1,0:T(8,128)} %fusion.104), kind=kOutput, calls=%fused_computation.133 | convolution fusion | flops 318514432 | bytes 16121856 | tf_op jit(solution)/shard_map/bkgqs,bqkgd->bskd/dot_general | solution.py:100
  429.2 3.3 add_convert_fusion.1
  432.4 10.8 %multiply_convert_fusion.1 = (bf16[4,256,1536]{2,1,0:T(8,128)(2,1)}, bf16[4,256,1536]{2,1,0:T(8,128)(2,1)}) fusion(f32[4,256,1536]{2,1,0:T(8,128)} %fusion.65, f32[4,256,1536]{2,1,0:T(8,128)} %get-tuple-element.70, bf16[4,256,576]{1,2,0:T(8,128)(2,1)} %add_convert_fusion.1, bf16[1,1536,576]{2,1,0:T(8,128)(2,1)} %all-gather.67.cloned.1.call-done), kind=kOutput, calls=%fused_computation.32 | convolution fusion | flops 1832386560 | bytes 21823488 | tf_op jit(solution)/shard_map/bsd,fd->bsf/dot_general | solution.py:77
  443.2 5.9 fusion.51
  449.1 7.7 multiply_reduce_fusion.1
  458.3 3.1 multiply_add_fusion
  465.1 5.1 fusion.101
  470.2 13.0 %fusion.78 = f32[4,256,3,64]{1,3,2,0:T(8,128)} fusion(bf16[4,256,3,3,64]{1,4,3,2,0:T(8,128)(2,1)} %pad_maximum_fusion, bf16[4,3,3,256,256]{3,4,2,1,0:T(8,128)(2,1)} %copy-done, f32[4,3,256,256,3]{3,2,4,1,0:T(8,128)} %fusion.101), kind=kOutput, calls=%fused_computation.134 | convolution fusion | flops 318514432 | bytes 16121856 | tf_op jit(solution)/shard_map/bkgqs,bqkgd->bskd/dot_general | solution.py:100
  488.0 4.2 fusion.80
  494.4 3.5 convolution_bitcast_fusion.8
  498.0 13.1 %fusion.18 = f32[4,3,64,3,256]{4,2,3,1,0:T(8,128)} fusion(bf16[4,3,3,256,256]{3,4,2,1,0:T(8,128)(2,1)} %copy-done, f32[4,3,256,256,3]{3,2,4,1,0:T(8,128)} %fusion.101, bf16[4,256,3,64]{1,3,2,0:T(8,128)(2,1)S(1)} %copy-done.58), kind=kOutput, calls=%fused_computation.38 | convolution fusion | flops 318514432 | bytes 16908288 | tf_op jit(solution)/shard_map/bkgqs,bskd->bqkgd/dot_general | solution.py:97
  516.8 4.5 convolution_bitcast_fusion.6
  523.7 6.0 convolution_bitcast_fusion.4
  531.0 5.6 convolution_bitcast_fusion.5
  536.7 6.0 convolution_bitcast_fusion.2
  542.8 5.7 convolution_bitcast_fusion.3
  549.7 6.4 convolution_bitcast_fusion
  557.5 6.5 convolution_bitcast_fusion.1
  564.7 11.7 %all-gather.34 = bf16[1,576,192]{2,1,0:T(8,128)(2,1)S(1)} all-gather(bf16[1,72,192]{2,1,0:T(8,128)(2,1)S(1)} %copy-done.61), channel_id=36, replica_groups=mesh['fsdp'=8] {'fsdp'}, dimensions={1}, use_global_device_ids=true | all-gather | bytes 248832 | tf_op jit(solution)/shard_map/all_gather | solution.py:119
  576.4 11.6 %all-gather.33 = bf16[1,576,192]{2,1,0:T(8,128)(2,1)S(1)} all-gather(bf16[1,72,192]{2,1,0:T(8,128)(2,1)S(1)} %copy-done.62), channel_id=35, replica_groups=mesh['fsdp'=8] {'fsdp'}, dimensions={1}, use_global_device_ids=true | all-gather | bytes 248832 | tf_op jit(solution)/shard_map/all_gather | solution.py:119
  587.9 14.1 %all-gather.32 = bf16[1,576,576]{2,1,0:T(8,128)(2,1)S(1)} all-gather(bf16[1,72,576]{2,1,0:T(8,128)(2,1)S(1)} %copy-done.60), channel_id=34, replica_groups=mesh['fsdp'=8] {'fsdp'}, dimensions={1}, use_global_device_ids=true | all-gather | bytes 746496 | tf_op jit(solution)/shard_map/all_gather | solution.py:119
  603.9 3.0 multiply_reduce_fusion.3
  606.9 22.7 %all-reduce.16 = (f32[576]{0:T(1024)}, f32[576]{0:T(1024)}, f32[576]{0:T(1024)}, f32[576]{0:T(1024)}) all-reduce(f32[576]{0:T(1024)S(1)} %get-tuple-element.93, f32[576]{0:T(1024)} %get-tuple-element.91, f32[576]{0:T(1024)} %get-tuple-element.89, f32[576]{0:T(1024)} %get-tuple-element.87), channel_id=53, replica_groups=mesh['fsdp'=8] {'fsdp'}, use_global_device_ids=true, to_apply=%region_31.32.clone | all-reduce | flops 2304 | bytes 18432
  632.3 3.3 add_convert_fusion
  640.6 29.6 %reduce-scatter.49.cloned.1.call-done = f32[72,576]{1,0:T(8,128)} async-done(((f32[576,576]{1,0:T(8,128)}), f32[72,576]{1,0:T(8,128)}) %reduce-scatter.49.cloned.1.call-update) | async-done | bytes 165904
  670.2 31.9 %reduce-scatter.47.cloned.1.call-done = f32[72,576]{1,0:T(8,128)} async-done(((f32[576,576]{1,0:T(8,128)}), f32[72,576]{1,0:T(8,128)}) %reduce-scatter.47.cloned.1.call-update) | async-done | bytes 165904
  703.9 41.0 %reduce-scatter.33.cloned.1.call-done = f32[72,1536]{1,0:T(8,128)} async-done(((f32[576,1536]{1,0:T(8,128)}), f32[72,1536]{1,0:T(8,128)}) %reduce-scatter.33.cloned.1.call-update) | async-done | bytes 442384 | tf_op jit(solution)/shard_map/reduce_scatter | solution.py:136
  744.9 42.8 %reduce-scatter.31.cloned.1.call-done = f32[72,1536]{1,0:T(8,128)} async-done(((f32[576,1536]{1,0:T(8,128)}), f32[72,1536]{1,0:T(8,128)}) %reduce-scatter.31.cloned.1.call-update) | async-done | bytes 442384 | tf_op jit(solution)/shard_map/reduce_scatter | solution.py:136
  789.8 40.7 %reduce-scatter.37.cloned.1.call-done = f32[72,1536]{1,0:T(8,128)} async-done(((f32[576,1536]{1,0:T(8,128)}), f32[72,1536]{1,0:T(8,128)}) %reduce-scatter.37.cloned.1.call-update) | async-done | bytes 442384 | tf_op jit(solution)/shard_map/reduce_scatter | solution.py:136
  830.4 42.6 %reduce-scatter.35.cloned.1.call-done = f32[72,1536]{1,0:T(8,128)} async-done(((f32[576,1536]{1,0:T(8,128)}), f32[72,1536]{1,0:T(8,128)}) %reduce-scatter.35.cloned.1.call-update) | async-done | bytes 442384 | tf_op jit(solution)/shard_map/reduce_scatter | solution.py:136
  875.2 42.5 %reduce-scatter.41.cloned.1.call-done = f32[192,576]{1,0:T(8,128)} async-done(((f32[1536,576]{1,0:T(8,128)}), f32[192,576]{1,0:T(8,128)}) %reduce-scatter.41.cloned.1.call-update) | async-done | bytes 442384 | tf_op jit(solution)/shard_map/reduce_scatter | solution.py:136
  917.7 44.5 %reduce-scatter.39.cloned.1.call-done = f32[192,576]{1,0:T(8,128)} async-done(((f32[1536,576]{1,0:T(8,128)}), f32[192,576]{1,0:T(8,128)}) %reduce-scatter.39.cloned.1.call-update) | async-done | bytes 442384 | tf_op jit(solution)/shard_map/reduce_scatter | solution.py:136
  (344 shorter events, 95.2 us)
Async XLA Ops:
  7.2 3.3 copy-start.20
  7.2 167.2 %all-gather.49.cloned.1.call-start = ((), (), s32[]{:S(2)}) async-start(), calls=%async_computation.24 | async-start | bytes 1990656 | tf_op jit(solution)/shard_map/all_gather | solution.py:119
  9.4 172.3 %all-gather.51.cloned.1.call-start = ((), (), s32[]{:S(2)}) async-start(), calls=%async_computation.25 | async-start | bytes 1990656 | tf_op jit(solution)/shard_map/all_gather | solution.py:119
  9.5 4.3 copy-start.4
  10.4 4.3 copy-start.70
  10.4 4.3 copy-start.68
  10.4 30.5 %copy-start.33 = (f32[2,72,576]{2,1,0:T(8,128)S(1)}, f32[2,72,576]{2,1,0:T(8,128)}, u32[]{:S(2)}) copy-start(f32[2,72,576]{2,1,0:T(8,128)} %param.13) | copy-start | bytes 995332
  10.4 182.0 %all-gather.53.cloned.1.call-start = ((), (), s32[]{:S(2)}) async-start(), calls=%async_computation.26 | async-start | bytes 2211840 | tf_op jit(solution)/shard_map/all_gather | solution.py:119
  10.5 48.2 %copy-start.57 = (f32[2,72,192]{2,1,0:T(8,128)S(1)}, f32[2,72,192]{2,1,0:T(8,128)}, u32[]{:S(2)}) copy-start(f32[2,72,192]{2,1,0:T(8,128)} %param.14) | copy-start | bytes 331780
  11.4 221.3 %all-gather.55.cloned.1.call-start = ((), (), s32[]{:S(2)}) async-start(), calls=%async_computation.27 | async-start | bytes 1990656 | tf_op jit(solution)/shard_map/all_gather | solution.py:119
  12.0 227.8 %all-gather.57.cloned.1.call-start = ((), (), s32[]{:S(2)}) async-start(), calls=%async_computation.28 | async-start | bytes 1990656 | tf_op jit(solution)/shard_map/all_gather | solution.py:119
  12.5 237.9 %all-gather.59.cloned.1.call-start = ((), (), s32[]{:S(2)}) async-start(), calls=%async_computation.29 | async-start | bytes 2211840 | tf_op jit(solution)/shard_map/all_gather | solution.py:119
  13.1 346.0 %all-gather.61.cloned.1.call-start = ((), (), s32[]{:S(2)}) async-start(), calls=%async_computation.30 | async-start | bytes 2211840 | tf_op jit(solution)/shard_map/all_gather | solution.py:119
  73.6 15.0 %copy-start.29 = (bf16[4,256,9,32]{1,3,2,0:T(8,128)(2,1)}, bf16[4,256,9,32]{1,3,2,0:T(8,128)(2,1)S(1)}, u32[]{:S(2)}) copy-start(bf16[4,256,9,32]{1,3,2,0:T(8,128)(2,1)S(1)} %get-tuple-element.118) | copy-start | bytes 1769476
  74.1 14.5 %copy-start.46 = (bf16[4,256,3,32]{1,3,2,0:T(8,128)(2,1)}, bf16[4,256,3,32]{1,3,2,0:T(8,128)(2,1)S(1)}, u32[]{:S(2)}) copy-start(bf16[4,256,3,32]{1,3,2,0:T(8,128)(2,1)S(1)} %get-tuple-element.125) | copy-start | bytes 589828
  74.1 14.5 %copy-start.47 = (bf16[4,256,3,32]{1,3,2,0:T(8,128)(2,1)}, bf16[4,256,3,32]{1,3,2,0:T(8,128)(2,1)S(1)}, u32[]{:S(2)}) copy-start(bf16[4,256,3,32]{1,3,2,0:T(8,128)(2,1)S(1)} %get-tuple-element.126) | copy-start | bytes 589828
  87.4 30.4 %copy-start.22 = (bf16[4,256,192]{1,2,0:T(8,128)(2,1)}, bf16[4,256,192]{1,2,0:T(8,128)(2,1)S(1)}, u32[]{:S(2)}) copy-start(bf16[4,256,192]{1,2,0:T(8,128)(2,1)S(1)} %convolution_convert_fusion.5) | copy-start | bytes 1179652
  119.9 28.8 %copy-start.63 = (bf16[1,72,192]{2,1,0:T(8,128)(2,1)S(1)}, bf16[1,72,192]{2,1,0:T(8,128)(2,1)}, u32[]{:S(2)}) copy-start(bf16[1,72,192]{2,1,0:T(8,128)(2,1)} %get-tuple-element.151) | copy-start | bytes 82948
  121.1 52.9 %copy-start.15 = (bf16[4,256,576]{1,2,0:T(8,128)(2,1)}, bf16[4,256,576]{1,2,0:T(8,128)(2,1)S(1)}, u32[]{:S(2)}) copy-start(bf16[4,256,576]{1,2,0:T(8,128)(2,1)S(1)} %get-tuple-element.72) | copy-start | bytes 3538948
  181.6 10.7 %copy-start.16 = (bf16[4,256,576]{1,2,0:T(8,128)(2,1)S(1)}, bf16[4,256,576]{1,2,0:T(8,128)(2,1)}, u32[]{:S(2)}) copy-start(bf16[4,256,576]{1,2,0:T(8,128)(2,1)} %copy-done.15) | copy-start | bytes 3538948
  202.1 14.9 %copy-start.24 = (bf16[4,256,192]{1,2,0:T(8,128)(2,1)}, bf16[4,256,192]{1,2,0:T(8,128)(2,1)S(1)}, u32[]{:S(2)}) copy-start(bf16[4,256,192]{1,2,0:T(8,128)(2,1)S(1)} %convolution_convert_fusion.4) | copy-start | bytes 1179652
  211.2 4.9 copy-start.48
  211.2 4.9 copy-start.49
  216.2 12.9 %copy-start.1 = (bf16[4,3,3,256,256]{3,4,2,1,0:T(8,128)(2,1)}, bf16[4,3,3,256,256]{3,4,2,1,0:T(8,128)(2,1)S(1)}, u32[]{:S(2)}) copy-start(bf16[4,3,3,256,256]{3,4,2,1,0:T(8,128)(2,1)S(1)} %divide_convert_fusion) | copy-start | bytes 14155780
  217.0 12.1 %copy-start.7 = (bf16[4,256,576]{1,2,0:T(8,128)(2,1)S(1)}, bf16[4,256,576]{1,2,0:T(8,128)(2,1)}, u32[]{:S(2)}) copy-start(bf16[4,256,576]{1,2,0:T(8,128)(2,1)} %copy-done.6) | copy-start | bytes 3538948
  217.0 12.1 %copy-start.52 = (bf16[1,576,576]{2,1,0:T(8,128)(2,1)S(1)}, bf16[1,576,576]{2,1,0:T(8,128)(2,1)}, u32[]{:S(2)}) copy-start(bf16[1,576,576]{2,1,0:T(8,128)(2,1)} %all-gather.13) | copy-start | bytes 1990660
  250.4 5.9 copy-start.21
  257.3 112.8 %all-gather.65.cloned.1.call-start = ((), (), s32[]{:S(2)}) async-start(), calls=%async_computation.32 | async-start | bytes 1990656 | tf_op jit(solution)/shard_map/all_gather | solution.py:119
  258.5 4.4 copy-start.69
  258.5 4.4 copy-start.71
  258.5 27.7 %copy-start.32 = (f32[2,72,576]{2,1,0:T(8,128)S(1)}, f32[2,72,576]{2,1,0:T(8,128)}, u32[]{:S(2)}) copy-start(f32[2,72,576]{2,1,0:T(8,128)} %param.16) | copy-start | bytes 995332
  258.6 27.7 %copy-start.56 = (f32[2,72,192]{2,1,0:T(8,128)S(1)}, f32[2,72,192]{2,1,0:T(8,128)}, u32[]{:S(2)}) copy-start(f32[2,72,192]{2,1,0:T(8,128)} %param.15) | copy-start | bytes 331780
  259.4 116.7 %all-gather.63.cloned.1.call-start = ((), (), s32[]{:S(2)}) async-start(), calls=%async_computation.31 | async-start | bytes 1990656 | tf_op jit(solution)/shard_map/all_gather | solution.py:119
  261.5 170.9 %all-gather.67.cloned.1.call-start = ((), (), s32[]{:S(2)}) async-start(), calls=%async_computation.33 | async-start | bytes 2211840 | tf_op jit(solution)/shard_map/all_gather | solution.py:119
  262.1 181.1 %all-gather.71.cloned.1.call-start = ((), (), s32[]{:S(2)}) async-start(), calls=%async_computation.35 | async-start | bytes 1990656 | tf_op jit(solution)/shard_map/all_gather | solution.py:119
  262.8 186.2 %all-gather.69.cloned.1.call-start = ((), (), s32[]{:S(2)}) async-start(), calls=%async_computation.34 | async-start | bytes 1990656 | tf_op jit(solution)/shard_map/all_gather | solution.py:119
  359.1 276.5 %reduce-scatter.25.cloned.1.call-start = ((), (), s32[]{:S(2)}) async-start(), calls=%async_computation.15 | async-start | bytes 663552 | tf_op jit(solution)/shard_map/reduce_scatter | solution.py:136
  370.1 17.5 %slice-start = ((s8[4718592]{0:T(1024)(128)(4,1)}), s8[524288]{0:T(1024)(128)(4,1)S(1)}, s32[]{:S(2)}) async-start(s8[4718592]{0:T(1024)(128)(4,1)} %bitcast.491), calls=%async_computation.40 | async-start | bytes 1048576
  376.1 6.6 copy-start.18
  376.1 6.6 copy-start.42
  376.1 11.5 %slice-start.1 = ((s8[4718592]{0:T(1024)(128)(4,1)}), s8[4194304]{0:T(1024)(128)(4,1)S(1)}, s32[]{:S(2)}) async-start(s8[4718592]{0:T(1024)(128)(4,1)} %bitcast.491), calls=%async_computation.41 | async-start | bytes 8388608
  389.1 5.1 copy-start.59
  443.2 5.9 copy-start.67
  458.1 177.5 %reduce-scatter.23.cloned.1.call-start = ((), (), s32[]{:S(2)}) async-start(), calls=%async_computation.14 | async-start | bytes 663552 | tf_op jit(solution)/shard_map/reduce_scatter | solution.py:136
  458.3 4.6 copy-start.50
  486.6 150.7 %reduce-scatter.29.cloned.1.call-start = ((), (), s32[]{:S(2)}) async-start(), calls=%async_computation.17 | async-start | bytes 663552 | tf_op jit(solution)/shard_map/reduce_scatter | solution.py:136
  487.9 149.3 %reduce-scatter.27.cloned.1.call-start = ((), (), s32[]{:S(2)}) async-start(), calls=%async_computation.16 | async-start | bytes 663552 | tf_op jit(solution)/shard_map/reduce_scatter | solution.py:136
  494.3 3.7 copy-start.58
  494.3 144.5 %reduce-scatter.45.cloned.1.call-start = ((), (), s32[]{:S(2)}) async-start(), calls=%async_computation.37 | async-start | bytes 1658880
  497.9 140.9 %reduce-scatter.43.cloned.1.call-start = ((), (), s32[]{:S(2)}) async-start(), calls=%async_computation.36 | async-start | bytes 1658880
  516.5 4.8 copy-start.3
  516.6 4.8 copy-start.13
  516.6 153.6 %reduce-scatter.49.cloned.1.call-start = ((), (), s32[]{:S(2)}) async-start(), calls=%async_computation.39 | async-start | bytes 1658880
  521.3 180.8 %reduce-scatter.47.cloned.1.call-start = ((), (), s32[]{:S(2)}) async-start(), calls=%async_computation.38 | async-start | bytes 1658880
  523.6 221.2 %reduce-scatter.33.cloned.1.call-start = ((), (), s32[]{:S(2)}) async-start(), calls=%async_computation.19 | async-start | bytes 3981312 | tf_op jit(solution)/shard_map/reduce_scatter | solution.py:136
  529.7 257.9 %reduce-scatter.31.cloned.1.call-start = ((), (), s32[]{:S(2)}) async-start(), calls=%async_computation.18 | async-start | bytes 3981312 | tf_op jit(solution)/shard_map/reduce_scatter | solution.py:136
  536.7 293.8 %reduce-scatter.37.cloned.1.call-start = ((), (), s32[]{:S(2)}) async-start(), calls=%async_computation.21 | async-start | bytes 3981312 | tf_op jit(solution)/shard_map/reduce_scatter | solution.py:136
  542.7 330.3 %reduce-scatter.35.cloned.1.call-start = ((), (), s32[]{:S(2)}) async-start(), calls=%async_computation.20 | async-start | bytes 3981312 | tf_op jit(solution)/shard_map/reduce_scatter | solution.py:136
  548.5 369.2 %reduce-scatter.41.cloned.1.call-start = ((), (), s32[]{:S(2)}) async-start(), calls=%async_computation.23 | async-start | bytes 4423680 | tf_op jit(solution)/shard_map/reduce_scatter | solution.py:136
  556.2 406.0 %reduce-scatter.39.cloned.1.call-start = ((), (), s32[]{:S(2)}) async-start(), calls=%async_computation.22 | async-start | bytes 4423680 | tf_op jit(solution)/shard_map/reduce_scatter | solution.py:136
  563.9 12.4 %copy-start.62 = (bf16[1,72,192]{2,1,0:T(8,128)(2,1)S(1)}, bf16[1,72,192]{2,1,0:T(8,128)(2,1)}, u32[]{:S(2)}) copy-start(bf16[1,72,192]{2,1,0:T(8,128)(2,1)} %get-tuple-element.149) | copy-start | bytes 82948
  563.9 24.0 %copy-start.60 = (bf16[1,72,576]{2,1,0:T(8,128)(2,1)S(1)}, bf16[1,72,576]{2,1,0:T(8,128)(2,1)}, u32[]{:S(2)}) copy-start(bf16[1,72,576]{2,1,0:T(8,128)(2,1)} %get-tuple-element.139) | copy-start | bytes 248836
  563.9 38.1 %copy-start.27 = (bf16[4,256,3,64]{1,3,2,0:T(8,128)(2,1)S(1)}, bf16[4,256,3,64]{1,3,2,0:T(8,128)(2,1)}, u32[]{:S(2)}) copy-start(bf16[4,256,3,64]{1,3,2,0:T(8,128)(2,1)} %copy-done.26) | copy-start | bytes 1179652
  564.0 38.6 %copy-start.40 = (bf16[4,256,9,64]{1,3,2,0:T(8,128)(2,1)S(1)}, bf16[4,256,9,64]{1,3,2,0:T(8,128)(2,1)}, u32[]{:S(2)}) copy-start(bf16[4,256,9,64]{1,3,2,0:T(8,128)(2,1)} %copy-done.39) | copy-start | bytes 3538948
  (36 other events, 52.8 us)
Sparse Core Ops, SparseCore 0:
  10.4 23.8 all-gather.48
  36.1 23.8 all-gather.50
  62.5 22.5 all-gather.52
  87.3 21.7 all-gather.54
  110.8 22.6 all-gather.56
  135.7 22.9 all-gather.58
  257.4 21.8 all-gather.60
  281.1 21.6 all-gather.64
  304.6 23.5 all-gather.62
  330.5 23.2 all-gather.66
  355.6 20.5 all-gather.70
  377.9 20.5 all-gather.68
  458.2 26.0 reduce-scatter.24
  487.8 26.0 reduce-scatter.22
  517.3 26.0 reduce-scatter.28
  546.2 26.0 reduce-scatter.26
  575.5 30.2 reduce-scatter.44
  608.9 29.1 reduce-scatter.42
  641.5 28.6 reduce-scatter.48
  673.4 28.6 reduce-scatter.46
  705.5 39.3 reduce-scatter.32
  748.3 39.3 reduce-scatter.30
  791.1 39.3 reduce-scatter.36
  833.7 39.3 reduce-scatter.34
  876.5 41.1 reduce-scatter.40
  921.0 41.1 reduce-scatter.38
where the time goes:
time: 980 us; the launch traced here: 971 us
  waiting for transfers between devices  319 us (33%)
  blocking collectives  285 us (29%)
  matrix products  265 us (27%)
  other arithmetic  59.1 us (6%)
  local copies, waits for them, and re-layouts  26.4 us (3%)
  between operations  15.9 us (2%)
    reduce_scatter x10, waiting for transfers between devices, local_step(): lax.psum_scatter(grad_full, 'fsdp', scatter_dimension=0, tiled=True)  254 us
    all_gather x16, blocking collectives, gather_layer(): lax.all_gather(master[layer_idx].astype(jnp.bfloat16), 'fsdp', axis=0, ti...  215 us
    unnamed x3, blocking collectives  70.4 us
    unnamed x30, waiting for transfers between devices  64.6 us
    dot_general x2, matrix products, layer_backward(): jnp.einsum('bkgqs,bskd->bqkgd', grad_scores, k_heads, preferred_element_t...  27.1 us
    dot_general x2, matrix products, layer_backward(): jnp.einsum('bkgqs,bqkgd->bskd', grad_scores, q_heads, preferred_element_t...  26.9 us
    dot_general x2, matrix products, layer_backward(): jnp.einsum('bsd,fd->bsf', grad_out, w_down, preferred_element_type=jnp.fl...  21.6 us
    dot_general x2, matrix products, layer_forward(): jnp.einsum('bsd,df->bsf', normed_mlp, w_up, preferred_element_type=jnp.fl...  21.3 us
  transfers between devices with their start and end apart: 26, of which 8 were waited for; matrix products, arithmetic and copies ran while one was open for 32% of the time, Pallas kernels for 0%

commit v1 on v0

v1 whole, which is shorter than its diff:
```python
import functools

import jax
import jax.numpy as jnp
from jax import lax
from jax.experimental import pallas as pl
from jax.experimental.pallas import tpu as pltpu
from jax.sharding import PartitionSpec as P

NORM_EPS = 1e-5
MASK_VALUE = -1e30
HEAD = 64
LAST = dict(axis=-1, keepdims=True)
KV_HEADS = 3
GROUP = 3
SEQ = 256
DIM = 576
FFN = 1536
QKV = 960
BF = jnp.bfloat16
F32 = jnp.float32


ROWS = ((1,), (1,))
COLS = ((0,), (0,))
PAIR = range(2)
HALF = SEQ // 2
LANES = 128
V_COL = DIM + KV_HEADS * HEAD


def origin(dims):
    return (0,) * len(dims)


def nth(width, index):
    return slice(width * index, width * (index + 1))


def dot(a, b, dims=((1,), (0,))):
    return lax.dot_general(a, b, (dims, ((), ())), preferred_element_type=F32)


def params(**kw):
    return pltpu.CompilerParams(dimension_semantics=("arbitrary",), vmem_limit_bytes=60 * 1024 * 1024, **kw)


def cost(flops, bytes_accessed):
    return pl.CostEstimate(flops=int(flops), bytes_accessed=int(bytes_accessed), transcendentals=0)


def shape(dims, dtype):
    return jax.ShapeDtypeStruct(dims, dtype)


def whole(dims):
    return pl.BlockSpec(dims, lambda i: origin(dims), pipeline_mode=pl.Buffered(1))


def rows(dims, base=0):
    return pl.BlockSpec((1,) + dims, lambda i: (i + base,) + origin(dims))


def one_of(dims, index):
    return pl.BlockSpec((1,) + dims, lambda i: (index,) + origin(dims), pipeline_mode=pl.Buffered(1))


def inv_rms(vals32):
    return lax.rsqrt(jnp.mean(vals32 * vals32, **LAST) + NORM_EPS)


def rms_back(vals32, inv, gain, grad_normed):
    scaled = vals32 * inv
    grad_scaled = grad_normed * gain
    grad_gain = jnp.sum(grad_normed * scaled, axis=0, keepdims=True)
    return inv * (grad_scaled - scaled * jnp.mean(grad_scaled * scaled, **LAST)), grad_gain


def rope(vals32, cos, sin):
    lane = lax.broadcasted_iota(jnp.int32, vals32.shape, 1)
    swapped = jnp.where(lane % HEAD < HEAD // 2, pltpu.roll(vals32, 96, 1), pltpu.roll(vals32, 32, 1))
    return vals32 * cos + swapped * sin


MESH = pl.DeviceIdType.MESH
ANY = pl.BlockSpec(memory_space=pl.ANY)


class Part:
    def __init__(self, x_first, r, c, stages, at, arrays=(), local=(), lo=0):
        self.x_first, self.r, self.c, self.stages, self.at = x_first, r, c, stages, at
        self.arrays, self.local, self.lo = list(arrays), list(local), lo
        full, two, one = (4, r, c), (2, r, c), (r, c)
        self.result = {"c": full, "a": two, "b": one}[stages[-1]]
        self.bufs = {}
        if "c" in stages:
            self.bufs["recv_c"] = full
            if not local:
                self.bufs["mine"] = full
        if "a" in stages:
            self.bufs["recv_a"] = two
        if "b" in stages:
            self.bufs["recv_b"] = one
        if stages[0] != "c":
            self.bufs["keep"] = two if stages[0] == "a" else one


class Gather:
    def __init__(self, x_first, r, c, srcs, specs, fill):
        self.x_first, self.r, self.c, self.srcs, self.specs, self.fill = x_first, r, c, srcs, specs, fill


def gather_of(x_first, layer, masters):
    widths = [m.shape[2] for m in masters]

    def fill(refs, dst):
        lo = 0
        for ref, width in zip(refs, widths):
            dst[:, lo:lo + width] = ref[0].astype(BF)
            lo += width

    specs = [pl.BlockSpec((1,) + m.shape[1:], lambda i: (layer, 0, 0)) for m in masters]
    return Gather(x_first, masters[0].shape[1], sum(widths), list(masters), specs, fill)


def gather_gains(gain_attn, gain_mlp):
    layers, r = gain_attn.shape

    def fill(refs, dst):
        dst[:] = jnp.zeros(dst.shape, BF)
        dst[0:layers, 0:r] = refs[0][:].astype(BF)
        dst[layers:2 * layers, 0:r] = refs[1][:].astype(BF)

    return Gather(True, 16, 128, [gain_attn, gain_mlp], [whole((layers, r))] * 2, fill)


def fused(body, steps, ins, in_specs, outs, out_specs, scratch, parts, cid, name, flops):
    n_in, n_out, n_scr, n_p = len(ins), len(outs), len(scratch), len(parts)
    comm = n_p > 0
    last = steps - 1

    def kernel(*refs):
        refs = list(refs)
        take = lambda k: [refs.pop(0) for _ in range(k)]
        in_refs = take(n_in)
        p_in = [take(len(p.arrays)) for p in parts]
        out_refs = take(n_out)
        p_out = take(n_p)
        scr = take(n_scr)
        p_scr = [dict(zip(p.bufs, take(len(p.bufs)))) for p in parts]
        step = pl.program_id(0)
        me = lax.axis_index("fsdp")
        core, x_bit, y_bit = lax.rem(me, 2), lax.rem(me // 2, 2), me // 4
        if not comm:
            body(step, last, core, in_refs, out_refs, scr)
            return
        (p_sem,) = take(1)
        pair, x_dev, y_dev = me + 1 - 2 * core, me + 2 - 4 * x_bit, me + 4 - 8 * y_bit

        def remote(src, dst, send, recv, dev):
            return pltpu.make_async_remote_copy(src_ref=src, dst_ref=dst, send_sem=send, recv_sem=recv, device_id=(dev,), device_id_type=MESH)

        def stages_of(t):
            part, bufs, arrays, out = parts[t], p_scr[t], p_in[t], p_out[t]
            sem = lambda k: p_sem.at[t, k]
            if part.x_first:
                sent, kept, dev_a, bit, dev_b = (lambda j: 2 * j + 1 - x_bit), (lambda j: 2 * j + x_bit), x_dev, y_bit, y_dev
            else:
                sent, kept, dev_a, bit, dev_b = (lambda j: 2 * (1 - y_bit) + j), (lambda j: 2 * y_bit + j), y_dev, x_bit, x_dev
            first, end = part.stages[0], part.stages[-1]
            span = pl.ds(part.lo, part.r)

            def copy_c():
                theirs = scr[part.local[1]] if part.local else arrays[1]
                return remote(theirs.at[:, span], bufs["recv_c"], sem(1), sem(2), pair)

            def copy_mine():
                return pltpu.make_async_copy(arrays[0].at[:, span], bufs["mine"], sem(0))

            def copy_a(j):
                src = arrays[0] if first == "a" else bufs["recv_c"]
                return remote(src.at[sent(j)], bufs["recv_a"].at[j], sem(3 + j), sem(5 + j), dev_a)

            def copy_keep(j):
                if first == "b":
                    return pltpu.make_async_copy(arrays[0].at[bit], bufs["keep"], sem(7))
                return pltpu.make_async_copy(arrays[0].at[kept(j)], bufs["keep"].at[j], sem(7 + j))

            def copy_b():
                src = arrays[0] if first == "b" else bufs["recv_a"]
                return remote(src.at[1 - bit], bufs["recv_b"], sem(9), sem(10), dev_b)

            def copy_out():
                return pltpu.make_async_copy(bufs["recv_" + end], out, sem(11))

            def mine_block(i):
                return scr[part.local[0]][i, part.lo:part.lo + part.r] if part.local else bufs["mine"][i]

            def begin():
                if first == "c":
                    copy_c().start()
                    if not part.local:
                        copy_mine().start()
                elif first == "a":
                    for j in PAIR:
                        copy_a(j).start()
                    for j in PAIR:
                        copy_keep(j).start()
                else:
                    copy_b().start()
                    copy_keep(0).start()

            def done_c():
                copy_c().wait()
                if not part.local:
                    copy_mine().wait()
                sums = bufs["recv_c"]
                for j in PAIR:
                    sums[sent(j)] = sums[sent(j)] + mine_block(sent(j))
                    if end != "c":
                        copy_a(j).start()
                for j in PAIR:
                    sums[kept(j)] = sums[kept(j)] + mine_block(kept(j))
                if end == "c":
                    copy_out().start()

            def done_a():
                for j in PAIR:
                    copy_a(j).wait()
                    if first == "a":
                        copy_keep(j).wait()
                for j in PAIR:
                    bufs["recv_a"][j] = bufs["recv_a"][j] + (bufs["keep"][j] if first == "a" else bufs["recv_c"][kept(j)])
                if end == "a":
                    copy_out().start()
                else:
                    copy_b().start()

            def done_b():
                copy_b().wait()
                if first == "b":
                    copy_keep(0).wait()
                bufs["recv_b"][:] = bufs["recv_b"][:] + (bufs["keep"][:] if first == "b" else bufs["recv_a"][bit])
                copy_out().start()

            calls = [begin] + [{"c": done_c, "a": done_a, "b": done_b}[stage] for stage in part.stages]
            return list(zip(part.at, calls)), copy_out

        def enter():
            barrier = pltpu.get_barrier_semaphore()
            for dev in (pair, x_dev, y_dev):
                pl.semaphore_signal(barrier, inc=1, device_id=(dev,), device_id_type=MESH)
            pl.semaphore_wait(barrier, 3)

        events = [(-1, enter)]
        outs_of = []
        for t in range(n_p):
            calls, copy_out = stages_of(t)
            events += calls
            outs_of.append(copy_out)
        events.sort(key=lambda event: event[0])

        def leave():
            for copy_out in outs_of:
                copy_out().wait()

        events.append((float("inf"), leave))
        if steps == 1:
            for _, call in events:
                call()
            return

        def at_step(lo, hi):
            calls = [call for at, call in events if lo <= at < hi]

            def run():
                for call in calls:
                    call()

            return run, len(calls)

        for index in range(steps):
            run, count = at_step(-1 if index == 0 else index, index + 1)
            if count:
                pl.when(step == index)(run)
        body(step, last, core, in_refs, out_refs, scr)
        pl.when(step == last)(at_step(steps, float("inf"))[0])
        pl.when(step == last)(leave)

    args = list(ins)
    in_specs, out_specs, outs, scratch = list(in_specs), list(out_specs), list(outs), list(scratch)
    for part in parts:
        args += part.arrays
        in_specs += [ANY] * len(part.arrays)
        outs.append(shape(part.result, F32))
        out_specs.append(ANY)
    for part in parts:
        scratch += [pltpu.VMEM(dims, F32) for dims in part.bufs.values()]
    extra = {}
    if comm:
        scratch += [pltpu.SemaphoreType.DMA((n_p, 12))]
        extra = dict(collective_id=cid, has_side_effects=True)
    return pl.pallas_call(
        kernel, grid=(steps,), in_specs=in_specs, out_specs=out_specs, out_shape=outs, scratch_shapes=scratch,
        compiler_params=params(**extra), cost_estimate=cost(flops, 2e7), name=name)(*args)


CHUNK = 512


def stack_heads(ref, kv, lo):
    return jnp.concatenate([ref[lo:lo + HALF, nth(HEAD, head)] for head in range(GROUP * kv, GROUP * (kv + 1))], axis=0)


P_DIMS = ((KV_HEADS, GROUP * HALF, HALF), (KV_HEADS, GROUP * HALF, SEQ))


def as_matrix(blocks):
    return blocks.reshape(8 * blocks.shape[1], blocks.shape[2])


class Ring:
    def __init__(self, me, ag, own, full, sems):
        self.me, self.ag, self.own, self.full, self.sems = me, ag, own, full, sems
        core, x_bit, y_bit = lax.rem(me, 2), lax.rem(me // 2, 2), me // 4
        self.pair, self.x_dev, self.y_dev = me + 1 - 2 * core, me + 2 - 4 * x_bit, me + 4 - 8 * y_bit

    def enter(self):
        barrier = pltpu.get_barrier_semaphore()
        for dev in (self.pair, self.x_dev, self.y_dev):
            pl.semaphore_signal(barrier, inc=1, device_id=(dev,), device_id_type=MESH)
        pl.semaphore_wait(barrier, 3)

    def copy(self, t, k):
        me, pair = self.me, self.pair
        one, two = (self.x_dev, self.y_dev) if self.ag[t].x_first else (self.y_dev, self.x_dev)
        blk = (me, me, me, one, one, two, one + two - me)[k]
        dev = (one, two, pair, two, pair, pair, pair)[k]
        src = self.own[t] if k < 3 else self.full[t].at[blk]
        return pltpu.make_async_remote_copy(src_ref=src, dst_ref=self.full[t].at[blk], send_sem=self.sems.at[t, k], recv_sem=self.sems.at[t, 7 + k], device_id=(dev,), device_id_type=MESH)

    def local(self, t):
        return pltpu.make_async_copy(self.own[t], self.full[t].at[self.me], self.sems.at[t, 14])

    def begin(self, group):
        for t in group:
            for k in range(3):
                self.copy(t, k).start()
            self.local(t).start()

    def forward(self, group):
        for t in group:
            self.copy(t, 0).wait_recv()
            self.copy(t, 3).start()
            self.copy(t, 4).start()
        for t in group:
            self.copy(t, 1).wait_recv()
            self.copy(t, 5).start()

    def end(self, group):
        for t in group:
            self.copy(t, 3).wait_recv()
            self.copy(t, 6).start()
        for t in group:
            for k in (2, 4, 5, 6):
                self.copy(t, k).wait_recv()
            for k in range(7):
                self.copy(t, k).wait_send()
            self.local(t).wait()


def attn_fwd_step(x32, wqkv, wo, gain, cos, sin, qkv_ref, p0_ref, p1_ref, o_ref):
    normed = (x32 * inv_rms(x32) * gain).astype(BF)
    proj = dot(normed, wqkv)
    for i in range(6):
        qkv_ref[0, :, nth(LANES, i)] = rope(proj[:, nth(LANES, i)], cos, sin).astype(BF)
    qkv_ref[0, :, V_COL:QKV] = proj[:, V_COL:QKV].astype(BF)
    half = HALF
    causal = lax.broadcasted_iota(jnp.int32, (GROUP * half, half), 0) % half >= lax.broadcasted_iota(jnp.int32, (GROUP * half, half), 1)
    for kv in range(KV_HEADS):
        keys = qkv_ref[0, :, DIM + HEAD * kv:DIM + HEAD * kv + HEAD]
        vals = qkv_ref[0, :, V_COL + HEAD * kv:V_COL + HEAD * kv + HEAD]
        for blk, p_ref in enumerate((p0_ref, p1_ref)):
            lo, length = half * blk, half * (blk + 1)
            s = dot(stack_heads(qkv_ref.at[0], kv, lo), keys[:length], ROWS) * HEAD ** -0.5
            diag = jnp.where(causal, s[:, lo:], MASK_VALUE)
            s = diag if blk == 0 else jnp.concatenate([s[:, :lo], diag], axis=1)
            e = jnp.exp(s - jnp.max(s, **LAST))
            p = (e * (1.0 / jnp.sum(e, **LAST))).astype(BF)
            p_ref[0, kv] = p
            o = dot(p, vals[:length]).astype(BF)
            for g in range(GROUP):
                head = GROUP * kv + g
                o_ref[0, lo:lo + half, nth(HEAD, head)] = o[nth(half, g)]
    return (x32 + dot(o_ref[0], wo)).astype(BF)


def forward(x_t, cos_t, sin_t, ag, cid):
    n = x_t.shape[0]
    n_g = len(ag)
    n_src = [len(g.srcs) for g in ag]
    head, mlp0, attn1, mlp1 = (0, 1, 2), (3, 4, 5), (6, 7), (8, 9, 10)

    def kernel(*refs):
        refs = list(refs)
        take = lambda k: [refs.pop(0) for _ in range(k)]
        x_ref, cos_ref, sin_ref = take(3)
        srcs = [take(k) for k in n_src]
        hid_ref, qkv_ref, p0_ref, p1_ref, o_ref, mid_ref, cos2_ref, sin2_ref, gains_ref = take(9)
        full = take(n_g)
        stream, mids, wqkv, wo, w1, w3, w2, g_all, act_ref = take(9)
        own = take(n_g)
        sems, load = take(2)
        step = pl.program_id(0)
        ring = Ring(lax.axis_index("fsdp"), ag, own, full, sems)

        def load_weights(pairs):
            copies = [pltpu.make_async_copy(full[t], dst, load.at[k]) for k, (t, dst) in enumerate(pairs)]
            for copy in copies:
                copy.start()
            for copy in copies:
                copy.wait()

        @pl.when(step == 0)
        def _():
            for t in head:
                ag[t].fill(srcs[t], own[t])
            ring.enter()
            ring.begin(head)
            for t in mlp0 + attn1 + mlp1:
                ag[t].fill(srcs[t], own[t])
            cos = cos_ref[:].T
            sin = sin_ref[:].T
            cos2_ref[:] = jnp.concatenate([cos] * 4, axis=1)
            sin2_ref[:] = jnp.concatenate([-sin, sin, -sin, sin], axis=1)
            ring.forward(head)
            ring.begin(mlp0)
            ring.end(head)
            load_weights([(0, wqkv), (1, wo), (2, g_all)])
            r = DIM // 8
            for d in range(8):
                for k in range(4):
                    gains_ref[k, :, nth(r, d)] = g_all[d, k:k + 1, :r].astype(F32)

        pl.when(step == n - 2)(lambda: ring.forward(mlp0[:2]))

        @pl.when(step == n - 1)
        def _():
            ring.forward(mlp0[2:])
            ring.begin(attn1)

        @pl.when(step == n)
        def _():
            ring.end(mlp0)
            load_weights([(3, w1), (4, w3), (5, w2)])

        @pl.when(step == n + 1)
        def _():
            ring.forward(attn1)
            ring.begin(mlp1)

        @pl.when(step == 2 * n)
        def _():
            ring.end(attn1)
            load_weights([(6, wqkv), (7, wo)])

        pl.when(step == 3 * n - 2)(lambda: ring.forward(mlp1[:2]))
        pl.when(step == 3 * n - 1)(lambda: ring.forward(mlp1[2:]))
        layer = step // (2 * n)
        seq = lax.rem(step, n)

        @pl.when(step < n)
        def _():
            stream[seq] = x_ref[0].T

        @pl.when((step < n) | (step >= 2 * n))
        def _():
            x = stream[seq]
            hid_ref[0] = x
            mid = attn_fwd_step(x.astype(F32), as_matrix(wqkv[:]), as_matrix(wo[:]), gains_ref[layer], cos2_ref[:], sin2_ref[:], qkv_ref, p0_ref, p1_ref, o_ref)
            mid_ref[0] = mid
            mids[seq] = mid

        @pl.when((step >= n) & (step < 2 * n))
        def _():
            h32 = mids[seq].astype(F32)
            normed = (h32 * inv_rms(h32) * gains_ref[2]).astype(BF)
            for c in range(0, FFN, CHUNK):
                gate = dot(normed, as_matrix(w1[:, :, c:c + CHUNK]))
                up = dot(normed, as_matrix(w3[:, :, c:c + CHUNK]))
                act_ref[:, c:c + CHUNK] = (gate * jax.nn.sigmoid(gate) * up).astype(BF)
            stream[seq] = (h32 + dot(act_ref[:], as_matrix(w2[:]))).astype(BF)

        pl.when(step == 3 * n - 1)(lambda: ring.end(mlp1))

    block = lambda i: jnp.where(i < n, i, jnp.where(i < 2 * n, n - 1, i - n))
    stacked = lambda dims: pl.BlockSpec((1,) + dims, lambda i: (block(i),) + origin(dims))
    saved = [(SEQ, DIM), (SEQ, QKV), P_DIMS[0], P_DIMS[1], (SEQ, DIM), (SEQ, DIM)]
    table = (SEQ, 2 * HEAD)
    bf_scratch = lambda dims: pltpu.VMEM(dims, BF)
    w_dims = [(8, ag[t].r, ag[t].c) for t in (0, 1, 3, 4, 5, 2)]
    return pl.pallas_call(
        kernel, grid=(3 * n,),
        in_specs=[pl.BlockSpec((1, DIM, SEQ), lambda i: (jnp.minimum(i, n - 1), 0, 0)), whole(cos_t.shape), whole(sin_t.shape)] + [spec for g in ag for spec in g.specs],
        out_specs=[stacked(dims) for dims in saved] + [whole(table), whole(table), whole((4, 1, DIM))] + [ANY] * n_g,
        out_shape=[shape((2 * n,) + dims, BF) for dims in saved] + [shape(table, F32), shape(table, F32), shape((4, 1, DIM), F32)] + [shape((8, g.r, g.c), BF) for g in ag],
        scratch_shapes=[bf_scratch((n, SEQ, DIM)), bf_scratch((n, SEQ, DIM))] + [bf_scratch(dims) for dims in w_dims] + [bf_scratch((SEQ, FFN))]
        + [bf_scratch((g.r, g.c)) for g in ag] + [pltpu.SemaphoreType.DMA((n_g, 15)), pltpu.SemaphoreType.DMA((3,))],
        compiler_params=params(collective_id=cid, has_side_effects=True), cost_estimate=cost(2e10, 4e7), name="forward",
    )(x_t, cos_t, sin_t, *[src for g in ag for src in g.srcs])


WIDE = 512
DOWN, GATE, UP = (6, 7), (8, 9), (10, 11)
TILES = FFN // WIDE


def mlp_bwd_body(step, last, core, ins, outs, scratch):
    h_ref, dy_ref, w1_ref, w3_ref, w2_ref, gain_ref = ins
    gm_ref, gg_ref, *y_ref = outs
    nt_ref, at_ref, act_ref, dgate_ref, dup_ref, dy_all, down_mine, down_theirs, gate_mine, gate_theirs, up_mine, up_theirs = scratch
    n = dy_all.shape[0] // SEQ
    gain = gain_ref[0]

    @pl.when(step < n)
    def _():
        h32 = h_ref[0].astype(F32)
        normed = (h32 * inv_rms(h32) * gain).astype(BF)
        tokens = pl.ds(pl.multiple_of(step * SEQ, SEQ), SEQ)
        nt_ref[:, tokens] = normed.T
        dy = dy_ref[0].T if y_ref else dy_ref[0]
        dy_all[tokens] = dy
        for c in range(0, FFN, CHUNK):
            cols = slice(c, c + CHUNK)
            gate = dot(normed, w1_ref[:, cols])
            up = dot(normed, w3_ref[:, cols])
            grad_act = dot(dy, w2_ref[cols, :], ROWS)
            sig = jax.nn.sigmoid(gate)
            silu = gate * sig
            act = (silu * up).astype(BF)
            if y_ref:
                act_ref[tokens, cols] = act
            at_ref[cols, tokens] = act.T
            dup_ref[tokens, cols] = (grad_act * silu).astype(BF)
            dgate_ref[tokens, cols] = (grad_act * up * sig * (1.0 + gate * (1.0 - sig))).astype(BF)

    @pl.when((step >= n) & (step < n + 4))
    def _():
        block = step - n
        span = 2 * FFN // 8
        full = dot(at_ref[pl.ds(pl.multiple_of(block * span, span), span)], dy_all[:])
        split_rows(full, core, down_mine.at[pl.ds(block, 1)], down_theirs.at[pl.ds(block, 1)])

    @pl.when((step >= n + 4) & (step < n + 4 + TILES))
    def _():
        cols = pl.ds(pl.multiple_of((step - n - 4) * WIDE, WIDE), WIDE)
        split_rows(dot(nt_ref[:], dgate_ref[:, cols]), core, gate_mine.at[:, :, cols], gate_theirs.at[:, :, cols])
        split_rows(dot(nt_ref[:], dup_ref[:, cols]), core, up_mine.at[:, :, cols], up_theirs.at[:, :, cols])

    @pl.when(step >= n + 4 + TILES)
    def _():
        tokens = pl.ds(pl.multiple_of((step - n - 4 - TILES) * SEQ, SEQ), SEQ)
        h32 = h_ref[0].astype(F32)
        if y_ref:
            y_ref[0][0] = (h32 + dot(act_ref[tokens], w2_ref[:])).astype(BF).T
        grad_normed = dot(dgate_ref[tokens], w1_ref[:], ROWS) + dot(dup_ref[tokens], w3_ref[:], ROWS)
        grad_h, grad_gain = rms_back(h32, inv_rms(h32), gain, grad_normed)
        gm_ref[0] = dy_all[tokens].astype(F32) + grad_h
        gg_ref[0] = grad_gain


def mlp_bwd(mid, dy, w1, w3, w2, gains, layer, with_out, parts, cid):
    n = dy.shape[0]
    base = layer * n
    tok = n * SEQ
    extra = 1 if with_out else 0
    r, rd = DIM // 8, FFN // 8
    tail = n + 4 + TILES
    steps = tail + n
    twice = pl.BlockSpec((1, SEQ, DIM), lambda i: (base + jnp.where(i < tail, jnp.minimum(i, n - 1), i - tail), 0, 0))
    early = pl.BlockSpec((1,) + dy.shape[1:], lambda i: (jnp.minimum(i, n - 1), 0, 0))
    late = lambda dims: pl.BlockSpec((1,) + dims, lambda i: (jnp.maximum(i - tail, 0),) + origin(dims))
    down_at = [n + 4, n + 6, steps]
    wide_at = [tail, steps]
    mine = [Part(True, rd // 2, DIM, "ca", down_at, local=DOWN), Part(False, rd // 2, DIM, "ca", down_at, local=DOWN, lo=rd // 2),
            Part(True, r, FFN, "c", wide_at, local=GATE), Part(False, r, FFN, "c", wide_at, local=UP)]
    return fused(
        mlp_bwd_body, steps, [mid, dy, w1, w3, w2, gains],
        [twice, early, whole(w1.shape), whole(w3.shape), whole(w2.shape), one_of((1, DIM), 2 + layer)],
        [shape((n, SEQ, DIM), F32), shape((n, 1, DIM), F32)] + [shape((n, DIM, SEQ), BF)] * extra,
        [late((SEQ, DIM)), late((1, DIM))] + [late((DIM, SEQ))] * extra,
        [pltpu.VMEM((DIM, tok), BF), pltpu.VMEM((FFN, tok), BF), pltpu.VMEM((tok if with_out else SEQ, FFN), BF), pltpu.VMEM((tok, FFN), BF), pltpu.VMEM((tok, FFN), BF), pltpu.VMEM((tok, DIM), BF)]
        + [pltpu.VMEM((4, rd, DIM), F32)] * 2 + [pltpu.VMEM((4, r, FFN), F32)] * 4,
        parts + mine, cid, "mlp_bwd", 2e10)


def split_rows(full, core, mine_ref, theirs_ref):
    blocks, r = mine_ref.shape[0], mine_ref.shape[1]

    @pl.when(core == 0)
    def _():
        for i in range(blocks):
            mine_ref[i] = full[2 * i * r:(2 * i + 1) * r]
            theirs_ref[i] = full[(2 * i + 1) * r:(2 * i + 2) * r]

    @pl.when(core == 1)
    def _():
        for i in range(blocks):
            theirs_ref[i] = full[2 * i * r:(2 * i + 1) * r]
            mine_ref[i] = full[(2 * i + 1) * r:(2 * i + 2) * r]


def attn_bwd_body(transposed, step, last, core, ins, outs, scratch):
    gm_ref, x_ref, qkv_ref, p0_ref, p1_ref, o_ref, wqkv_ref, wo_ref, gain_ref, cos_ref, sin_ref = ins
    dx_ref, gg_ref, qkv_mine, qkv_theirs, out_mine, out_theirs = outs
    do_ref, dqk_ref, dqkv_ref, acc_qkv, acc_out = scratch
    gm = gm_ref[0]
    gmb = gm.astype(BF)
    x32 = x_ref[0].astype(F32)
    inv = inv_rms(x32)
    gain = gain_ref[0]
    normed = (x32 * inv * gain).astype(BF)
    do_ref[:] = dot(gmb, wo_ref[:], ROWS).astype(BF)
    half = HALF
    for kv in range(KV_HEADS):
        kcol = DIM + HEAD * kv
        vcol = V_COL + HEAD * kv
        keys = qkv_ref[0, :, kcol:kcol + HEAD]
        vals = qkv_ref[0, :, vcol:vcol + HEAD]
        dk, dv = [], []
        for blk, p_ref in enumerate((p0_ref, p1_ref)):
            lo, length = half * blk, half * (blk + 1)
            p = p_ref[0, kv]
            d_o = stack_heads(do_ref, kv, lo)
            q = stack_heads(qkv_ref.at[0], kv, lo)
            dp = dot(d_o, vals[:length], ROWS)
            p32 = p.astype(F32)
            ds = (p32 * (dp - jnp.sum(p32 * dp, **LAST)) * HEAD ** -0.5).astype(BF)
            dq = dot(ds, keys[:length])
            for g in range(GROUP):
                head = GROUP * kv + g
                dqk_ref[lo:lo + half, nth(HEAD, head)] = dq[nth(half, g)]
            dk.append(dot(q, ds, COLS))
            dv.append(dot(d_o, p, COLS))
        dk, dv = [jnp.concatenate([a[0] + a[1][:, :half], a[1][:, half:]], axis=1).T for a in (dk, dv)]
        dqk_ref[:, kcol:kcol + HEAD] = dk
        dqkv_ref[:, vcol:vcol + HEAD] = dv.astype(BF)
    cos, sin = cos_ref[:], -sin_ref[:]
    for i in range(6):
        cols = nth(LANES, i)
        dqkv_ref[:, cols] = rope(dqk_ref[:, cols], cos, sin).astype(BF)
    grad_normed = dot(dqkv_ref[:], wqkv_ref[:], ROWS)
    grad_x, grad_gain = rms_back(x32, inv, gain, grad_normed)
    dx = (gm + grad_x).astype(BF)
    dx_ref[0] = dx.T if transposed else dx
    gg_ref[0] = grad_gain
    part_qkv = dot(normed, dqkv_ref[:], COLS)
    part_out = dot(o_ref[0], gmb, COLS)

    @pl.when(step == 0)
    def _():
        acc_qkv[:] = part_qkv
        acc_out[:] = part_out

    @pl.when(step > 0)
    def _():
        acc_qkv[:] += part_qkv
        acc_out[:] += part_out

    @pl.when(step == last)
    def _():
        split_rows(acc_qkv, core, qkv_mine, qkv_theirs)
        split_rows(acc_out, core, out_mine, out_theirs)


def attn_bwd(gm, saved, wqkv, wo, gains, cos, sin, layer, parts, cid):
    hid, qkv, p0, p1, o = saved
    n = gm.shape[0]
    base = layer * n
    r = DIM // 8
    dx, dx_spec = (shape((n, SEQ, DIM), BF), rows((SEQ, DIM))) if layer else (shape((n, DIM, SEQ), BF), rows((DIM, SEQ)))
    return fused(
        functools.partial(attn_bwd_body, layer == 0), n, [gm, hid, qkv, p0, p1, o, wqkv, wo, gains, cos, sin],
        [rows((SEQ, DIM)), rows((SEQ, DIM), base), rows((SEQ, QKV), base), rows(P_DIMS[0], base), rows(P_DIMS[1], base), rows((SEQ, DIM), base), whole(wqkv.shape), whole(wo.shape), one_of((1, DIM), layer), whole(cos.shape), whole(sin.shape)],
        [dx, shape((n, 1, DIM), F32), shape((4, r, QKV), F32), shape((4, r, QKV), F32), shape((4, r, DIM), F32), shape((4, r, DIM), F32)],
        [dx_spec, rows((1, DIM)), whole((4, r, QKV)), whole((4, r, QKV)), whole((4, r, DIM)), whole((4, r, DIM))],
        [pltpu.VMEM((SEQ, DIM), BF), pltpu.VMEM((SEQ, 768), F32), pltpu.VMEM((SEQ, QKV), BF), pltpu.VMEM((DIM, QKV), F32), pltpu.VMEM((DIM, DIM), F32)],
        parts, cid, "attn_bwd", 1e10)


def pick(stacked, index, axis):
    return lax.dynamic_index_in_dim(stacked, index, axis, keepdims=False)


def solution(mesh):
    shard_spec = P(None, "fsdp")
    batch_spec = P("fsdp")

    def local_step(w_query, w_key, w_value, w_out, w_gate, w_up, w_down, gain_attn, gain_mlp, rope_cos, rope_sin, x_in, y_cot):
        me = lax.axis_index("fsdp")
        bits = (me % 2, (me // 2) % 2, me // 4)
        num_layers = w_query.shape[0]
        attn_ag = lambda i: [gather_of(False, i, (w_query, w_key, w_value)), gather_of(True, i, (w_out,))]
        mlp_ag = lambda i: [gather_of(True, i, (w_gate,)), gather_of(False, i, (w_up,)), gather_of(i == 0, i, (w_down,))]
        merge = lambda v: v.reshape(-1, v.shape[2])
        ag = attn_ag(0) + [gather_gains(gain_attn, gain_mlp)] + mlp_ag(0) + attn_ag(1) + mlp_ag(1)
        hid, qkv, p0, p1, attn, mid, cos, sin, gains, *full = forward(jnp.swapaxes(x_in, 1, 2), rope_cos.T, rope_sin.T, ag, 2 * num_layers + 1)
        full = [merge(v) for v in full]
        weights = [full[:2] + full[3:6], full[6:]]
        grad = jnp.swapaxes(y_cot, 1, 2)
        grads = [None] * num_layers
        gain_grads = []
        y_out = None
        r, rd = w_query.shape[1], w_down.shape[1]
        done = {}
        wide, heads = [], []
        for i in reversed(range(num_layers)):
            qkv_w, out_w, gate_w, up_w, down_w = weights[i]
            last = i == num_layers - 1
            seqs = x_in.shape[0]
            at_b = [0, seqs + 4]
            at_cab = [0, 2, seqs + 4, 2 * seqs + 4 + TILES]
            parts = [Part(first == 0, r, width, "cab", at_cab, arrays=pair) for first, (width, pair) in enumerate(heads)]
            parts = [Part(first == 0, r, FFN, "b", at_b, arrays=[v]) for first, v in enumerate(wide)] + parts
            res = mlp_bwd(mid, grad, gate_w, up_w, down_w, gains, i, last, parts, 2 * i)
            gm, gg2 = res[:2]
            if last:
                y_out = res[2]
            rest = res[3 if last else 2:]
            done[i + 1] = list(rest[:len(parts)])
            down0, down1, gate_s, up_s = rest[len(parts):]
            parts = [Part(True, r, FFN, "a", [0, seqs], arrays=[gate_s]), Part(False, r, FFN, "a", [0, seqs], arrays=[up_s]),
                     Part(True, rd // 2, DIM, "b", [0, seqs], arrays=[down0]), Part(False, rd // 2, DIM, "b", [0, seqs], arrays=[down1])]
            res = attn_bwd(gm, (hid, qkv, p0, p1, attn), qkv_w, out_w, gains, cos, sin, i, parts, 2 * i + 1)
            grad, gg1, q_mine, q_theirs, o_mine, o_theirs = res[:6]
            wide = list(res[6:8])
            done[i, "down"] = res[8:10]
            heads = [(QKV, [q_mine, q_theirs]), (DIM, [o_mine, o_theirs])]
            gain_grads = [gg1.sum((0, 1)), gg2.sum((0, 1))] + gain_grads
        gsum = jnp.stack(gain_grads).reshape(2 * num_layers, 4, 2, r)
        gsum = jnp.pad(gsum.transpose(2, 1, 0, 3).reshape(2, 4, 2 * num_layers * r), ((0, 0), (0, 0), (0, 1024 - 2 * num_layers * r))).reshape(2, 4, 8, 128)
        parts = [Part(first == 0, r, FFN, "b", [1.5, 4], arrays=[v]) for first, v in enumerate(wide)]
        parts += [Part(first == 0, r, width, "cab", [0, 1, 2, 3], arrays=pair) for first, (width, pair) in enumerate(heads)]
        parts += [Part(True, 8, 128, "cab", [0, 1, 2, 3], arrays=[pick(gsum, bits[0], 0), pick(gsum, 1 - bits[0], 0)])]
        *done[0], gain_sums = fused(None, 1, [], [], [], [], [], parts, 2 * num_layers, "rs_tail", 1e6)
        s_gains = gain_sums.reshape(1024)[:2 * num_layers * r].reshape(2 * num_layers, r)
        for i in range(num_layers):
            s_gate, s_up, s_qkv, s_out = done[i]
            down0, down1 = done[i, "down"]
            grads[i] = (s_qkv[:, :576], s_qkv[:, 576:768], s_qkv[:, 768:960], s_out, s_gate, s_up, jnp.concatenate([down0, down1], 0))
        stacked = tuple(jnp.stack(parts) for parts in zip(*grads))
        return (jnp.swapaxes(y_out, 1, 2), jnp.swapaxes(grad, 1, 2)) + stacked + (s_gains[0::2], s_gains[1::2])

    in_specs = (shard_spec,) * 9 + (P(), P(), batch_spec, batch_spec)
    out_specs = (batch_spec, batch_spec) + (shard_spec,) * 9
    return jax.shard_map(local_step, mesh=mesh, in_specs=in_specs, out_specs=out_specs, check_vma=False)
```

time: 980 us -> 282 us (0.29)
  waiting for transfers between devices: 319 us -> 0 us
  blocking collectives: 285 us -> 0 us
  Pallas kernels: 0 us -> 267 us
  matrix products: 265 us -> 0 us
  other arithmetic: 59.1 us -> 8.31 us
  local copies, waits for them, and re-layouts: 26.4 us -> 5.11 us
  between operations: 15.9 us -> 0.89 us
    pallas_call x0 -> x6, Pallas kernels: none -> 267 us  [the longest x5 186 us: fused(): pl.pallas_call(kernel, grid=(steps,), in_specs=in_specs, out_specs=out_sp...]
    reduce_scatter x10 -> x0, waiting for transfers between devices: 254 us -> none  [local_step(): lax.psum_scatter(grad_full, 'fsdp', scatter_dimension=0, tiled=True)]
    dot_general x52 -> x0, matrix products: 248 us -> none  [the longest x2 27.1 us: layer_backward(): jnp.einsum('bkgqs,bskd->bqkgd', grad_scores, k_heads, preferred_element_t...]
    all_gather x16 -> x0, blocking collectives: 215 us -> none  [gather_layer(): lax.all_gather(master[layer_idx].astype(jnp.bfloat16), 'fsdp', axis=0, ti...]
    unnamed x3 -> x0, blocking collectives: 70.4 us -> none
    unnamed x30 -> x0, waiting for transfers between devices: 64.6 us -> none
    another operation x35 -> x6, other arithmetic: 28.5 us -> 6.81 us  [local_step(): stacked = tuple((jnp.stack(parts) for parts in zip(*grads)))]
    convert_element_type x16 -> x0, other arithmetic: 18.6 us -> none  [the longest x2 9.78 us: layer_forward(): attn_probs = jax.nn.softmax(scores, axis=-1).astype(jnp.bfloat16)]
  transfers between devices with their start and end apart: 26 -> 0, of which waited for: 8 -> 0; matrix products, arithmetic and copies ran while one was open for 32% -> 0% of each run, Pallas kernels for 0% -> 0%
where the time goes in v1:
time: 282 us
  Pallas kernels  267 us (95%)
  other arithmetic  8.31 us (3%)
  local copies, waits for them, and re-layouts  5.11 us (2%)
    pallas_call x5, Pallas kernels, fused(): pl.pallas_call(kernel, grid=(steps,), in_specs=in_specs, out_specs=out_sp...  186 us
    pallas_call x1, Pallas kernels, forward(): pl.pallas_call(kernel, grid=(3 * n,), in_specs=[pl.BlockSpec((1, DIM, SEQ...  81.5 us
    another operation x6, other arithmetic, local_step(): stacked = tuple((jnp.stack(parts) for parts in zip(*grads)))  6.81 us

profile of v1, /device:TPU:0, one launch (start us, length us, event | category | flops | bytes accessed | tf_op | source)
XLA Modules:
  0.0 281.6 jit_solution(753385395724809698)
XLA Ops:
  0.7 81.5 %forward.1 = (bf16[8,256,576]{2,1,0:T(8,128)(2,1)}, bf16[8,256,960]{2,1,0:T(8,128)(2,1)}, bf16[8,3,384,128]{3,2,1,0:T(8,128)(2,1)}, bf16[8,3,384,256]{3,2,1,0:T(...) custom-call(bf16[4,576,256]{2,1,0:T(8,128)(2,1)} %bitcast.54, ...), custom_call_target="tpu_custom_call" | custom-call | flops 20000000000 | bytes 40000000 | tf_op jit(solution)/shard_map/forward/pallas_call | solution.py:502
  82.2 37.9 %mlp_bwd.2 = (f32[4,256,576]{2,1,0:T(8,128)}, f32[4,1,576]{2,1,0:T(1,128)}, bf16[4,576,256]{2,1,0:T(8,128)(2,1)}, f32[2,96,576]{2,1,0:T(8,128)}, f32[2,96,576]{2...) custom-call(bf16[8,256,576]{2,1,0:T(8,128)(2,1)} %get-tuple-element.72.refs_0_, ...), custom_call_target="tpu_custom_call" | custom-call | flops 20000000000 | bytes 20000000 | tf_op jit(solution)/shard_map/mlp_bwd/pallas_call | solution.py:303
  120.1 0.7 reduce_sum.39
  120.8 0.1 stack.81
  120.9 33.1 %attn_bwd.2 = (bf16[4,256,576]{2,1,0:T(8,128)(2,1)}, f32[4,1,576]{2,1,0:T(1,128)}, f32[4,72,960]{2,1,0:T(8,128)}, f32[4,72,960]{2,1,0:T(8,128)}, f32[4,72,576]{2...) custom-call(f32[4,256,576]{2,1,0:T(8,128)} %get-tuple-element.78.ref, ...), custom_call_target="tpu_custom_call" | custom-call | flops 10000000000 | bytes 20000000 | tf_op jit(solution)/shard_map/attn_bwd/pallas_call | solution.py:303
  154.0 48.9 %mlp_bwd.3 = (f32[4,256,576]{2,1,0:T(8,128)}, f32[4,1,576]{2,1,0:T(1,128)}, f32[72,1536]{1,0:T(8,128)}, f32[72,1536]{1,0:T(8,128)}, f32[72,960]{1,0:T(8,128)}, /...) custom-call(bf16[8,256,576]{2,1,0:T(8,128)(2,1)} %get-tuple-element., ...), custom_call_target="tpu_custom_call" | custom-call | flops 20000000000 | bytes 20000000 | tf_op jit(solution)/shard_map/mlp_bwd/pallas_call | solution.py:303
  202.9 0.0 copy-start.12
  202.9 0.0 copy-start.11
  202.9 32.3 %attn_bwd.3 = (bf16[4,576,256]{2,1,0:T(8,128)(2,1)}, f32[4,1,576]{2,1,0:T(1,128)}, f32[4,72,960]{2,1,0:T(8,128)}, f32[4,72,960]{2,1,0:T(8,128)}, f32[4,72,576]{2...) custom-call(f32[4,256,576]{2,1,0:T(8,128)} %get-tuple-element.102.re, ...), custom_call_target="tpu_custom_call" | custom-call | flops 10000000000 | bytes 20000000 | tf_op jit(solution)/shard_map/attn_bwd/pallas_call | solution.py:303
  235.3 0.7 reduce_sum.36
  236.0 0.1 stack.78
  236.1 0.0 copy-done.12
  236.1 0.1 stack.79
  236.2 0.0 copy-done.11
  236.2 0.1 stack.80
  236.4 0.1 reshape.83
  236.5 0.6 dynamic-slice_bitcast_fusion
  237.1 0.0 copy-start.10
  237.1 0.0 copy-start.2
  237.1 0.0 copy-start.3
  237.1 33.6 %rs_tail.1 = (f32[72,1536]{1,0:T(8,128)}, f32[72,1536]{1,0:T(8,128)}, f32[72,960]{1,0:T(8,128)}, f32[72,576]{1,0:T(8,128)}, f32[8,128]{1,0:T(8,128)}) custom-call(f32[2,72,1536]{2,1,0:T(8,128)} %get-tuple-element.110.refs_0_, f32[2,72,1536]{2,1,0:T(8,128)} %get-tuple-element.111.refs_1_, f32[4,72,960]{2,1,0:T(8,128)} %get-tuple-element.112.refs_2_, ...), custom_call_target="tpu_custom_call" | custom-call | flops 1000000 | bytes 20000000 | tf_op jit(solution)/shard_map/rs_tail/pallas_call | solution.py:303
  270.7 0.0 copy-done.10
  270.7 1.7 pad_maximum_fusion.4
  272.4 0.0 copy-done.2
  272.4 0.0 copy-done.3
  272.4 0.0 copy-start.13
  272.4 0.0 copy-start.5
  272.4 0.0 copy-start.4
  272.4 2.5 pad_maximum_fusion.1
  274.9 0.0 copy-start.6
  275.0 0.0 copy-start.7
  275.0 0.0 copy-start.8
  275.0 0.0 copy-start.9
  275.0 0.0 copy-done.13
  275.0 0.1 reshape.86
  275.1 0.6 slice.35
  275.7 0.6 slice.34
  276.2 0.0 copy-done.5
  276.2 0.1 slice_bitcast_fusion.3
  276.3 0.0 copy-done.4
  276.4 0.1 slice_bitcast_fusion.2
  276.4 0.8 pad_maximum_fusion.3
  277.2 0.7 pad_maximum_fusion.5
  277.9 0.0 copy-done.6
  277.9 0.0 copy-done.7
  278.0 0.0 copy-done.8
  278.0 0.0 copy-done.9
  278.0 0.0 copy-start
  278.0 0.1 maximum_bitcast_fusion
  278.1 0.0 copy-start.1
  278.1 1.0 pad_maximum_fusion
  279.1 0.5 copy-done
  279.6 1.0 copy.27
  280.6 0.0 copy-done.1
  280.6 1.0 copy.28
  (8 shorter events, 0.1 us)
Async XLA Ops:
  202.9 33.2 %copy-start.12 = (f32[4,1,576]{2,1,0:T(1,128)S(1)}, f32[4,1,576]{2,1,0:T(1,128)}, u32[]{:S(2)}) copy-start(f32[4,1,576]{2,1,0:T(1,128)} %get-tuple-element.117) | copy-start | bytes 27652
  202.9 33.3 %copy-start.11 = (f32[4,1,576]{2,1,0:T(1,128)S(1)}, f32[4,1,576]{2,1,0:T(1,128)}, u32[]{:S(2)}) copy-start(f32[4,1,576]{2,1,0:T(1,128)} %get-tuple-element.118) | copy-start | bytes 27652
  237.1 33.6 %copy-start.10 = (f32[72,576]{1,0:T(8,128)S(1)}, f32[72,576]{1,0:T(8,128)}, u32[]{:S(2)}) copy-start(f32[72,576]{1,0:T(8,128)} %get-tuple-element.123) | copy-start | bytes 497668
  237.1 35.3 %copy-start.2 = (f32[72,1536]{1,0:T(8,128)S(1)}, f32[72,1536]{1,0:T(8,128)}, u32[]{:S(2)}) copy-start(f32[72,1536]{1,0:T(8,128)} %get-tuple-element.125) | copy-start | bytes 1327108
  237.1 35.3 %copy-start.3 = (f32[72,1536]{1,0:T(8,128)S(1)}, f32[72,1536]{1,0:T(8,128)}, u32[]{:S(2)}) copy-start(f32[72,1536]{1,0:T(8,128)} %get-tuple-element.127) | copy-start | bytes 1327108
  272.4 2.6 copy-start.13
  272.4 3.8 %copy-start.5 = (f32[72,960]{1,0:T(8,128)S(1)}, f32[72,960]{1,0:T(8,128)}, u32[]{:S(2)}) copy-start(f32[72,960]{1,0:T(8,128)} %get-tuple-element.120) | copy-start | bytes 829444
  272.4 3.9 %copy-start.4 = (f32[72,960]{1,0:T(8,128)S(1)}, f32[72,960]{1,0:T(8,128)}, u32[]{:S(2)}) copy-start(f32[72,960]{1,0:T(8,128)} %get-tuple-element.121) | copy-start | bytes 829444
  274.9 3.0 %copy-start.6 = (f32[96,576]{1,0:T(8,128)S(1)}, f32[96,576]{1,0:T(8,128)}, u32[]{:S(2)}) copy-start(f32[96,576]{1,0:T(8,128)} %get-tuple-element.130) | copy-start | bytes 663556
  275.0 3.0 %copy-start.7 = (f32[96,576]{1,0:T(8,128)S(1)}, f32[96,576]{1,0:T(8,128)}, u32[]{:S(2)}) copy-start(f32[96,576]{1,0:T(8,128)} %get-tuple-element.131) | copy-start | bytes 663556
  275.0 3.0 %copy-start.8 = (f32[96,576]{1,0:T(8,128)S(1)}, f32[96,576]{1,0:T(8,128)}, u32[]{:S(2)}) copy-start(f32[96,576]{1,0:T(8,128)} %get-tuple-element.128) | copy-start | bytes 663556
  275.0 3.0 %copy-start.9 = (f32[96,576]{1,0:T(8,128)S(1)}, f32[96,576]{1,0:T(8,128)}, u32[]{:S(2)}) copy-start(f32[96,576]{1,0:T(8,128)} %get-tuple-element.129) | copy-start | bytes 663556
  278.0 1.6 copy-start
  278.1 2.6 copy-start.1

commit v2 on v1

--- a/solution.py
+++ b/solution.py
@@ -26,6 +26,7 @@
 PAIR = range(2)
 HALF = SEQ // 2
 LANES = 128
+VMEM_BYTES = 66 * 10 ** 6
 V_COL = DIM + KV_HEADS * HEAD
 
 
@@ -42,7 +43,7 @@
 
 
 def params(**kw):
-    return pltpu.CompilerParams(dimension_semantics=("arbitrary",), vmem_limit_bytes=60 * 1024 * 1024, **kw)
+    return pltpu.CompilerParams(dimension_semantics=("arbitrary",), vmem_limit_bytes=VMEM_BYTES, **kw)
 
 
 def cost(flops, bytes_accessed):
@@ -515,10 +516,10 @@
 TILES = FFN // WIDE
 
 
-def mlp_bwd_body(step, last, core, ins, outs, scratch):
+def mlp_bwd_body(step, core, ins, outs, scratch):
     h_ref, dy_ref, w1_ref, w3_ref, w2_ref, gain_ref = ins
-    gm_ref, gg_ref, *y_ref = outs
-    nt_ref, at_ref, act_ref, dgate_ref, dup_ref, dy_all, down_mine, down_theirs, gate_mine, gate_theirs, up_mine, up_theirs = scratch
+    gg_ref, *y_ref = outs
+    nt_ref, at_ref, act_ref, dgate_ref, dup_ref, dy_all, down_mine, down_theirs, gate_mine, gate_theirs, up_mine, up_theirs, gm_ref = scratch
     n = dy_all.shape[0] // SEQ
     gain = gain_ref[0]
 
@@ -557,7 +558,7 @@
         split_rows(dot(nt_ref[:], dgate_ref[:, cols]), core, gate_mine.at[:, :, cols], gate_theirs.at[:, :, cols])
         split_rows(dot(nt_ref[:], dup_ref[:, cols]), core, up_mine.at[:, :, cols], up_theirs.at[:, :, cols])
 
-    @pl.when(step >= n + 4 + TILES)
+    @pl.when((step >= n + 4 + TILES) & (step < n + 4 + TILES + n))
     def _():
         tokens = pl.ds(pl.multiple_of((step - n - 4 - TILES) * SEQ, SEQ), SEQ)
         h32 = h_ref[0].astype(F32)
@@ -565,33 +566,8 @@
             y_ref[0][0] = (h32 + dot(act_ref[tokens], w2_ref[:])).astype(BF).T
         grad_normed = dot(dgate_ref[tokens], w1_ref[:], ROWS) + dot(dup_ref[tokens], w3_ref[:], ROWS)
         grad_h, grad_gain = rms_back(h32, inv_rms(h32), gain, grad_normed)
-        gm_ref[0] = dy_all[tokens].astype(F32) + grad_h
+        gm_ref[step - n - 4 - TILES] = dy_all[tokens].astype(F32) + grad_h
         gg_ref[0] = grad_gain
-
-
-def mlp_bwd(mid, dy, w1, w3, w2, gains, layer, with_out, parts, cid):
-    n = dy.shape[0]
-    base = layer * n
-    tok = n * SEQ
-    extra = 1 if with_out else 0
-    r, rd = DIM // 8, FFN // 8
-    tail = n + 4 + TILES
-    steps = tail + n
-    twice = pl.BlockSpec((1, SEQ, DIM), lambda i: (base + jnp.where(i < tail, jnp.minimum(i, n - 1), i - tail), 0, 0))
-    early = pl.BlockSpec((1,) + dy.shape[1:], lambda i: (jnp.minimum(i, n - 1), 0, 0))
-    late = lambda dims: pl.BlockSpec((1,) + dims, lambda i: (jnp.maximum(i - tail, 0),) + origin(dims))
-    down_at = [n + 4, n + 6, steps]
-    wide_at = [tail, steps]
-    mine = [Part(True, rd // 2, DIM, "ca", down_at, local=DOWN), Part(False, rd // 2, DIM, "ca", down_at, local=DOWN, lo=rd // 2),
-            Part(True, r, FFN, "c", wide_at, local=GATE), Part(False, r, FFN, "c", wide_at, local=UP)]
-    return fused(
-        mlp_bwd_body, steps, [mid, dy, w1, w3, w2, gains],
-        [twice, early, whole(w1.shape), whole(w3.shape), whole(w2.shape), one_of((1, DIM), 2 + layer)],
-        [shape((n, SEQ, DIM), F32), shape((n, 1, DIM), F32)] + [shape((n, DIM, SEQ), BF)] * extra,
-        [late((SEQ, DIM)), late((1, DIM))] + [late((DIM, SEQ))] * extra,
-        [pltpu.VMEM((DIM, tok), BF), pltpu.VMEM((FFN, tok), BF), pltpu.VMEM((tok if with_out else SEQ, FFN), BF), pltpu.VMEM((tok, FFN), BF), pltpu.VMEM((tok, FFN), BF), pltpu.VMEM((tok, DIM), BF)]
-        + [pltpu.VMEM((4, rd, DIM), F32)] * 2 + [pltpu.VMEM((4, r, FFN), F32)] * 4,
-        parts + mine, cid, "mlp_bwd", 2e10)
 
 
 def split_rows(full, core, mine_ref, theirs_ref):
@@ -610,11 +586,10 @@
             mine_ref[i] = full[(2 * i + 1) * r:(2 * i + 2) * r]
 
 
-def attn_bwd_body(transposed, step, last, core, ins, outs, scratch):
-    gm_ref, x_ref, qkv_ref, p0_ref, p1_ref, o_ref, wqkv_ref, wo_ref, gain_ref, cos_ref, sin_ref = ins
+def attn_bwd_body(transposed, step, last, core, gm, ins, outs, scratch):
+    x_ref, qkv_ref, p0_ref, p1_ref, o_ref, wqkv_ref, wo_ref, gain_ref, cos_ref, sin_ref = ins
     dx_ref, gg_ref, qkv_mine, qkv_theirs, out_mine, out_theirs = outs
-    do_ref, dqk_ref, dqkv_ref, acc_qkv, acc_out = scratch
-    gm = gm_ref[0]
+    do_ref, dqk_ref, dqkv_ref, acc_qkv, acc_out, sems = scratch
     gmb = gm.astype(BF)
     x32 = x_ref[0].astype(F32)
     inv = inv_rms(x32)
@@ -649,12 +624,12 @@
     for i in range(6):
         cols = nth(LANES, i)
         dqkv_ref[:, cols] = rope(dqk_ref[:, cols], cos, sin).astype(BF)
-    grad_normed = dot(dqkv_ref[:], wqkv_ref[:], ROWS)
+    grad_normed = dot(dqkv_ref[:, :QKV], wqkv_ref[:], ROWS)
     grad_x, grad_gain = rms_back(x32, inv, gain, grad_normed)
     dx = (gm + grad_x).astype(BF)
     dx_ref[0] = dx.T if transposed else dx
     gg_ref[0] = grad_gain
-    part_qkv = dot(normed, dqkv_ref[:], COLS)
+    part_qkv = dot(normed, dqkv_ref[:, :QKV], COLS)
     part_out = dot(o_ref[0], gmb, COLS)
 
     @pl.when(step == 0)
@@ -669,23 +644,63 @@
 
     @pl.when(step == last)
     def _():
-        split_rows(acc_qkv, core, qkv_mine, qkv_theirs)
-        split_rows(acc_out, core, out_mine, out_theirs)
-
-
-def attn_bwd(gm, saved, wqkv, wo, gains, cos, sin, layer, parts, cid):
+        copies = []
+        for acc, mine, theirs in ((acc_qkv, qkv_mine, qkv_theirs), (acc_out, out_mine, out_theirs)):
+            r = mine.shape[1]
+            for dst, side in ((mine, core), (theirs, 1 - core)):
+                for i in range(4):
+                    src = acc.at[pl.ds(pl.multiple_of((2 * i + side) * r, 8), r)]
+                    copies.append(pltpu.make_async_copy(src, dst.at[i], sems.at[len(copies)]))
+        for copy in copies:
+            copy.start()
+        for copy in copies:
+            copy.wait()
+
+
+def layer_bwd(mid, dy, saved, weights, gains, cos, sin, layer, with_out, parts, cid):
     hid, qkv, p0, p1, o = saved
-    n = gm.shape[0]
+    wqkv, wo, w1, w3, w2 = weights
+    n = dy.shape[0]
     base = layer * n
-    r = DIM // 8
-    dx, dx_spec = (shape((n, SEQ, DIM), BF), rows((SEQ, DIM))) if layer else (shape((n, DIM, SEQ), BF), rows((DIM, SEQ)))
+    tok = n * SEQ
+    extra = 1 if with_out else 0
+    r, rd = DIM // 8, FFN // 8
+    tail = n + 4 + TILES
+    head = tail + n
+    steps = head + n
+
+    def body(step, last, core, ins, outs, scratch):
+        mid_ref, dy_ref, w1_ref, w3_ref, w2_ref, gain_ref, *attn_ins = ins
+        dx_ref, gg_attn, q_mine, q_theirs, o_mine, o_theirs, *mlp_outs = outs
+        mlp_scratch, (dqk, acc_qkv, acc_out, sems) = scratch[:-4], scratch[-4:]
+        attn_scratch = mlp_scratch[5].at[:SEQ], dqk, mlp_scratch[3].at[:SEQ], acc_qkv, acc_out, sems
+        mlp_bwd_body(step, core, (mid_ref, dy_ref, w1_ref, w3_ref, w2_ref, gain_ref), mlp_outs, mlp_scratch)
+
+        @pl.when(step >= head)
+        def _():
+            gm = mlp_scratch[-1][step - head]
+            attn_bwd_body(layer == 0, step - head, n - 1, core, gm, attn_ins, (dx_ref, gg_attn, q_mine, q_theirs, o_mine, o_theirs), attn_scratch)
+
+    def block(dims, first, offset=0):
+        return pl.BlockSpec((1,) + dims, lambda i: (offset + jnp.clip(i - first, 0, n - 1),) + origin(dims))
+
+    twice = pl.BlockSpec((1, SEQ, DIM), lambda i: (base + jnp.where(i < tail, jnp.minimum(i, n - 1), jnp.minimum(i - tail, n - 1)), 0, 0))
+    down_at = [n + 4, n + 6, head + 1, steps]
+    wide_at = [tail, tail + 2, steps]
+    mine = [Part(True, rd // 2, DIM, "cab", down_at, local=DOWN), Part(False, rd // 2, DIM, "cab", down_at, local=DOWN, lo=rd // 2),
+            Part(True, r, FFN, "ca", wide_at, local=GATE), Part(False, r, FFN, "ca", wide_at, local=UP)]
+    dx = (DIM, SEQ) if layer == 0 else (SEQ, DIM)
+    halves = [(4, r, QKV)] * 2 + [(4, r, DIM)] * 2
     return fused(
-        functools.partial(attn_bwd_body, layer == 0), n, [gm, hid, qkv, p0, p1, o, wqkv, wo, gains, cos, sin],
-        [rows((SEQ, DIM)), rows((SEQ, DIM), base), rows((SEQ, QKV), base), rows(P_DIMS[0], base), rows(P_DIMS[1], base), rows((SEQ, DIM), base), whole(wqkv.shape), whole(wo.shape), one_of((1, DIM), layer), whole(cos.shape), whole(sin.shape)],
-        [dx, shape((n, 1, DIM), F32), shape((4, r, QKV), F32), shape((4, r, QKV), F32), shape((4, r, DIM), F32), shape((4, r, DIM), F32)],
-        [dx_spec, rows((1, DIM)), whole((4, r, QKV)), whole((4, r, QKV)), whole((4, r, DIM)), whole((4, r, DIM))],
-        [pltpu.VMEM((SEQ, DIM), BF), pltpu.VMEM((SEQ, 768), F32), pltpu.VMEM((SEQ, QKV), BF), pltpu.VMEM((DIM, QKV), F32), pltpu.VMEM((DIM, DIM), F32)],
-        parts, cid, "attn_bwd", 1e10)
+        body, steps, [mid, dy, w1, w3, w2, gains, hid, qkv, p0, p1, o, wqkv, wo, gains, cos, sin],
+        [twice, block(dy.shape[1:], 0), whole(w1.shape), whole(w3.shape), whole(w2.shape), one_of((1, DIM), 2 + layer)]
+        + [block(v.shape[1:], head, base) for v in saved] + [whole(wqkv.shape), whole(wo.shape), one_of((1, DIM), layer), whole(cos.shape), whole(sin.shape)],
+        [shape((n,) + dx, BF), shape((n, 1, DIM), F32)] + [shape(dims, F32) for dims in halves] + [shape((n, 1, DIM), F32)] + [shape((n, DIM, SEQ), BF)] * extra,
+        [block(dx, head), block((1, DIM), head)] + [ANY] * 4 + [block((1, DIM), tail)] + [block((DIM, SEQ), tail)] * extra,
+        [pltpu.VMEM((DIM, tok), BF), pltpu.VMEM((FFN, tok), BF), pltpu.VMEM((tok, FFN) if with_out else (16, LANES), BF), pltpu.VMEM((tok, FFN), BF), pltpu.VMEM((tok, FFN), BF), pltpu.VMEM((tok, DIM), BF)]
+        + [pltpu.VMEM((4, rd, DIM), F32)] * 2 + [pltpu.VMEM((4, r, FFN), F32)] * 4 + [pltpu.VMEM((n, SEQ, DIM), F32)]
+        + [pltpu.VMEM((SEQ, V_COL), F32), pltpu.VMEM((DIM, QKV), F32), pltpu.VMEM((DIM, DIM), F32), pltpu.SemaphoreType.DMA((16,))],
+        parts + mine, cid, "layer_bwd", 3e10)
 
 
 def pick(stacked, index, axis):
@@ -715,26 +730,20 @@
         done = {}
         wide, heads = [], []
         for i in reversed(range(num_layers)):
-            qkv_w, out_w, gate_w, up_w, down_w = weights[i]
             last = i == num_layers - 1
             seqs = x_in.shape[0]
             at_b = [0, seqs + 4]
-            at_cab = [0, 2, seqs + 4, 2 * seqs + 4 + TILES]
-            parts = [Part(first == 0, r, width, "cab", at_cab, arrays=pair) for first, (width, pair) in enumerate(heads)]
-            parts = [Part(first == 0, r, FFN, "b", at_b, arrays=[v]) for first, v in enumerate(wide)] + parts
-            res = mlp_bwd(mid, grad, gate_w, up_w, down_w, gains, i, last, parts, 2 * i)
-            gm, gg2 = res[:2]
+            at_cab = [0, 2, seqs + 5, 2 * seqs + 4 + TILES]
+            parts = [Part(first == 0, r, FFN, "b", at_b, arrays=[v]) for first, v in enumerate(wide)]
+            parts += [Part(first == 0, r, width, "cab", at_cab, arrays=pair) for first, (width, pair) in enumerate(heads)]
+            res = layer_bwd(mid, grad, (hid, qkv, p0, p1, attn), weights[i], gains, cos, sin, i, last, parts, i)
+            grad, gg1, q_mine, q_theirs, o_mine, o_theirs, gg2 = res[:7]
             if last:
-                y_out = res[2]
-            rest = res[3 if last else 2:]
+                y_out = res[7]
+            rest = res[8 if last else 7:]
             done[i + 1] = list(rest[:len(parts)])
-            down0, down1, gate_s, up_s = rest[len(parts):]
-            parts = [Part(True, r, FFN, "a", [0, seqs], arrays=[gate_s]), Part(False, r, FFN, "a", [0, seqs], arrays=[up_s]),
-                     Part(True, rd // 2, DIM, "b", [0, seqs], arrays=[down0]), Part(False, rd // 2, DIM, "b", [0, seqs], arrays=[down1])]
-            res = attn_bwd(gm, (hid, qkv, p0, p1, attn), qkv_w, out_w, gains, cos, sin, i, parts, 2 * i + 1)
-            grad, gg1, q_mine, q_theirs, o_mine, o_theirs = res[:6]
-            wide = list(res[6:8])
-            done[i, "down"] = res[8:10]
+            done[i, "down"] = rest[len(parts):len(parts) + 2]
+            wide = list(rest[len(parts) + 2:])
             heads = [(QKV, [q_mine, q_theirs]), (DIM, [o_mine, o_theirs])]
             gain_grads = [gg1.sum((0, 1)), gg2.sum((0, 1))] + gain_grads
         gsum = jnp.stack(gain_grads).reshape(2 * num_layers, 4, 2, r)

time: 282 us -> 266 us (0.943)
  Pallas kernels: 267 us -> 253 us
    pallas_call x5 -> x3, Pallas kernels: 186 us -> 171 us  [fused(): pl.pallas_call(kernel, grid=(steps,), in_specs=in_specs, out_specs=out_sp...]
where the time goes in v2:
time: 266 us
  Pallas kernels  253 us (95%)
  other arithmetic  7.05 us (3%)
  local copies, waits for them, and re-layouts  4.6 us (2%)
    pallas_call x3, Pallas kernels, fused(): pl.pallas_call(kernel, grid=(steps,), in_specs=in_specs, out_specs=out_sp...  171 us
    pallas_call x1, Pallas kernels, forward(): pl.pallas_call(kernel, grid=(3 * n,), in_specs=[pl.BlockSpec((1, DIM, SEQ...  81.5 us
    another operation x6, other arithmetic, local_step(): stacked = tuple((jnp.stack(parts) for parts in zip(*grads)))  6.95 us

profile of v2, /device:TPU:0, one launch (start us, length us, event | category | flops | bytes accessed | tf_op | source)
XLA Modules:
  0.0 265.5 jit_solution(1886013529294013357)
XLA Ops:
  0.6 81.5 %forward.1 = (bf16[8,256,576]{2,1,0:T(8,128)(2,1)}, bf16[8,256,960]{2,1,0:T(8,128)(2,1)}, bf16[8,3,384,128]{3,2,1,0:T(8,128)(2,1)}, bf16[8,3,384,256]{3,2,1,0:T(...) custom-call(bf16[4,576,256]{2,1,0:T(8,128)(2,1)} %bitcast.54, ...), custom_call_target="tpu_custom_call" | custom-call | flops 20000000000 | bytes 40000000 | tf_op jit(solution)/shard_map/forward/pallas_call | solution.py:503
  82.2 63.8 %layer_bwd.2 = (bf16[4,256,576]{2,1,0:T(8,128)(2,1)}, f32[4,1,576]{2,1,0:T(1,128)}, f32[4,72,960]{2,1,0:T(8,128)}, f32[4,72,960]{2,1,0:T(8,128)}, f32[4,72,576]{...) custom-call(bf16[8,256,576]{2,1,0:T(8,128)(2,1)} %get-tuple-element., ...), custom_call_target="tpu_custom_call" | custom-call | flops 30000001024 | bytes 20000000 | tf_op jit(solution)/shard_map/layer_bwd/pallas_call | solution.py:304
  146.0 0.0 copy-start.6
  146.0 0.0 copy-start.7
  146.0 74.1 %layer_bwd.3 = (bf16[4,576,256]{2,1,0:T(8,128)(2,1)}, f32[4,1,576]{2,1,0:T(1,128)}, f32[4,72,960]{2,1,0:T(8,128)}, f32[4,72,960]{2,1,0:T(8,128)}, f32[4,72,576]{...) custom-call(bf16[8,256,576]{2,1,0:T(8,128)(2,1)} %get-tuple-element., ...), custom_call_target="tpu_custom_call" | custom-call | flops 30000001024 | bytes 20000000 | tf_op jit(solution)/shard_map/layer_bwd/pallas_call | solution.py:304
  220.1 0.0 copy-done.6
  220.1 0.0 copy-done.7
  220.1 1.1 maximum_bitcast_fusion
  221.3 0.0 copy-start.13
  221.3 0.0 copy-start.12
  221.3 0.0 copy-start.11
  221.3 0.0 copy-start.10
  221.3 1.0 pad_maximum_fusion
  222.3 0.0 copy-done.13
  222.4 0.1 stack.78
  222.4 0.0 copy-done.12
  222.5 0.1 stack.79
  222.6 0.0 copy-done.11
  222.6 0.1 stack.80
  222.7 0.0 copy-done.10
  222.7 0.1 stack.81
  222.8 0.1 reshape.83
  223.0 0.6 dynamic-slice_bitcast_fusion
  223.6 0.0 copy-start.2
  223.6 0.0 copy-start.3
  223.6 33.5 %rs_tail.1 = (f32[72,1536]{1,0:T(8,128)}, f32[72,1536]{1,0:T(8,128)}, f32[72,960]{1,0:T(8,128)}, f32[72,576]{1,0:T(8,128)}, f32[8,128]{1,0:T(8,128)}) custom-call(f32[2,72,1536]{2,1,0:T(8,128)} %get-tuple-element.90.refs_0_, f32[2,72,1536]{2,1,0:T(8,128)} %get-tuple-element.91.refs_1_, f32[4,72,960]{2,1,0:T(8,128)} %get-tuple-element.92.refs_2_, ...), custom_call_target="tpu_custom_call" | custom-call | flops 1000000 | bytes 20000000 | tf_op jit(solution)/shard_map/rs_tail/pallas_call | solution.py:304
  257.1 0.0 copy-done.2
  257.2 0.0 copy-done.3
  257.2 0.0 copy-start.8
  257.2 0.0 copy-start.9
  257.2 0.0 copy-start.5
  257.2 0.0 copy-start.4
  257.2 2.5 pad_maximum_fusion.1
  259.7 0.0 copy-done.8
  259.8 0.0 copy-done.9
  259.8 0.8 pad_maximum_fusion.4
  260.5 0.0 copy-done.5
  260.5 0.0 copy-start.14
  260.5 0.0 copy-start
  260.5 0.1 slice_bitcast_fusion.3
  260.6 0.0 copy-done.4
  260.6 0.1 slice_bitcast_fusion.2
  260.7 0.7 pad_maximum_fusion.5
  261.5 0.8 pad_maximum_fusion.3
  262.2 0.0 copy-start.1
  262.2 0.0 copy-done.14
  262.2 0.1 reshape.86
  262.3 0.6 slice.34
  262.9 0.6 slice.35
  263.5 0.0 copy-done
  263.5 1.0 copy.27
  264.5 0.0 copy-done.1
  264.5 1.0 copy.28
  (10 shorter events, 0.2 us)
Async XLA Ops:
  146.0 74.1 %copy-start.6 = (f32[96,576]{1,0:T(8,128)S(1)}, f32[96,576]{1,0:T(8,128)}, u32[]{:S(2)}) copy-start(f32[96,576]{1,0:T(8,128)} %get-tuple-element.110) | copy-start | bytes 663556
  146.0 74.1 %copy-start.7 = (f32[96,576]{1,0:T(8,128)S(1)}, f32[96,576]{1,0:T(8,128)}, u32[]{:S(2)}) copy-start(f32[96,576]{1,0:T(8,128)} %get-tuple-element.111) | copy-start | bytes 663556
  221.3 1.1 copy-start.13
  221.3 1.2 copy-start.12
  221.3 1.3 copy-start.11
  221.3 1.4 copy-start.10
  223.6 33.6 %copy-start.2 = (f32[72,1536]{1,0:T(8,128)S(1)}, f32[72,1536]{1,0:T(8,128)}, u32[]{:S(2)}) copy-start(f32[72,1536]{1,0:T(8,128)} %get-tuple-element.105) | copy-start | bytes 1327108
  223.6 33.6 %copy-start.3 = (f32[72,1536]{1,0:T(8,128)S(1)}, f32[72,1536]{1,0:T(8,128)}, u32[]{:S(2)}) copy-start(f32[72,1536]{1,0:T(8,128)} %get-tuple-element.107) | copy-start | bytes 1327108
  257.2 2.6 copy-start.8
  257.2 2.6 copy-start.9
  257.2 3.3 %copy-start.5 = (f32[72,960]{1,0:T(8,128)S(1)}, f32[72,960]{1,0:T(8,128)}, u32[]{:S(2)}) copy-start(f32[72,960]{1,0:T(8,128)} %get-tuple-element.100) | copy-start | bytes 829444
  257.2 3.4 %copy-start.4 = (f32[72,960]{1,0:T(8,128)S(1)}, f32[72,960]{1,0:T(8,128)}, u32[]{:S(2)}) copy-start(f32[72,960]{1,0:T(8,128)} %get-tuple-element.101) | copy-start | bytes 829444
  260.5 1.7 copy-start.14
  260.5 3.0 %copy-start = (bf16[4,576,256]{2,1,0:T(8,128)(2,1)S(1)}, bf16[4,576,256]{2,1,0:T(8,128)(2,1)}, u32[]{:S(2)}) copy-start(bf16[4,576,256]{2,1,0:T(8,128)(2,1)} %get-tuple-element.76) | copy-start | bytes 3538948
  262.2 2.3 copy-start.1

commit v3 on v2

--- a/solution.py
+++ b/solution.py
@@ -443,7 +443,9 @@
                 for k in range(4):
                     gains_ref[k, :, nth(r, d)] = g_all[d, k:k + 1, :r].astype(F32)
 
-        pl.when(step == n - 2)(lambda: ring.forward(mlp0[:2]))
+        @pl.when(step == n - 2)
+        def _():
+            ring.forward(mlp0[:2])
 
         @pl.when(step == n - 1)
         def _():
@@ -453,20 +455,31 @@
         @pl.when(step == n)
         def _():
             ring.end(mlp0)
+            ring.begin(mlp1[:1])
             load_weights([(3, w1), (4, w3), (5, w2)])
 
         @pl.when(step == n + 1)
         def _():
             ring.forward(attn1)
-            ring.begin(mlp1)
+            ring.begin(mlp1[1:])
 
         @pl.when(step == 2 * n)
         def _():
             ring.end(attn1)
             load_weights([(6, wqkv), (7, wo)])
 
-        pl.when(step == 3 * n - 2)(lambda: ring.forward(mlp1[:2]))
-        pl.when(step == 3 * n - 1)(lambda: ring.forward(mlp1[2:]))
+        @pl.when(step == 2 * n + 1)
+        def _():
+            ring.forward(mlp1[:1])
+
+        @pl.when(step == 3 * n - 2)
+        def _():
+            ring.forward(mlp1[1:2])
+
+        @pl.when(step == 3 * n - 1)
+        def _():
+            ring.forward(mlp1[2:])
+
         layer = step // (2 * n)
         seq = lax.rem(step, n)
 
@@ -703,6 +716,28 @@
         parts + mine, cid, "layer_bwd", 3e10)
 
 
+def pack_kernel(*refs):
+    layers = refs[:6], refs[6:12]
+    gain_sums, y_ref, dx_ref, wq, wk, wv, wo, wg, wu, wd, g1, g2, y_out, dx_out = refs[12:]
+    y_out[:] = y_ref[:]
+    dx_out[:] = dx_ref[:]
+    for i, (gate, up, qkv, out, down0, down1) in enumerate(layers):
+        wq[i], wk[i], wv[i] = qkv[:, :DIM], qkv[:, DIM:DIM + wk.shape[2]], qkv[:, DIM + wk.shape[2]:]
+        wo[i], wg[i], wu[i] = out[:], gate[:], up[:]
+        g1[i:i + 1] = gain_sums[2 * i:2 * i + 1, :g1.shape[1]]
+        g2[i:i + 1] = gain_sums[2 * i + 1:2 * i + 2, :g2.shape[1]]
+        half = down0.shape[0]
+        wd[i, :half] = down0[:]
+        wd[i, half:] = down1[:]
+
+
+def pack(parts, shapes):
+    vmem = pl.BlockSpec(memory_space=pltpu.VMEM)
+    return pl.pallas_call(
+        pack_kernel, in_specs=[vmem] * len(parts), out_specs=[vmem] * len(shapes), out_shape=shapes,
+        compiler_params=pltpu.CompilerParams(vmem_limit_bytes=VMEM_BYTES), cost_estimate=cost(1e6, 7e6), name="pack")(*parts)
+
+
 def pick(stacked, index, axis):
     return lax.dynamic_index_in_dim(stacked, index, axis, keepdims=False)
 
@@ -723,7 +758,6 @@
         full = [merge(v) for v in full]
         weights = [full[:2] + full[3:6], full[6:]]
         grad = jnp.swapaxes(y_cot, 1, 2)
-        grads = [None] * num_layers
         gain_grads = []
         y_out = None
         r, rd = w_query.shape[1], w_down.shape[1]
@@ -746,19 +780,16 @@
             wide = list(rest[len(parts) + 2:])
             heads = [(QKV, [q_mine, q_theirs]), (DIM, [o_mine, o_theirs])]
             gain_grads = [gg1.sum((0, 1)), gg2.sum((0, 1))] + gain_grads
-        gsum = jnp.stack(gain_grads).reshape(2 * num_layers, 4, 2, r)
-        gsum = jnp.pad(gsum.transpose(2, 1, 0, 3).reshape(2, 4, 2 * num_layers * r), ((0, 0), (0, 0), (0, 1024 - 2 * num_layers * r))).reshape(2, 4, 8, 128)
+        gsum = jnp.stack(gain_grads).reshape(-1, 4, 2, r).transpose(2, 1, 0, 3)
+        gsum = jnp.pad(gsum, ((0, 0), (0, 0), (0, 8 - gsum.shape[2]), (0, LANES - r)))
         parts = [Part(first == 0, r, FFN, "b", [1.5, 4], arrays=[v]) for first, v in enumerate(wide)]
         parts += [Part(first == 0, r, width, "cab", [0, 1, 2, 3], arrays=pair) for first, (width, pair) in enumerate(heads)]
         parts += [Part(True, 8, 128, "cab", [0, 1, 2, 3], arrays=[pick(gsum, bits[0], 0), pick(gsum, 1 - bits[0], 0)])]
         *done[0], gain_sums = fused(None, 1, [], [], [], [], [], parts, 2 * num_layers, "rs_tail", 1e6)
-        s_gains = gain_sums.reshape(1024)[:2 * num_layers * r].reshape(2 * num_layers, r)
-        for i in range(num_layers):
-            s_gate, s_up, s_qkv, s_out = done[i]
-            down0, down1 = done[i, "down"]
-            grads[i] = (s_qkv[:, :576], s_qkv[:, 576:768], s_qkv[:, 768:960], s_out, s_gate, s_up, jnp.concatenate([down0, down1], 0))
-        stacked = tuple(jnp.stack(parts) for parts in zip(*grads))
-        return (jnp.swapaxes(y_out, 1, 2), jnp.swapaxes(grad, 1, 2)) + stacked + (s_gains[0::2], s_gains[1::2])
+        masters = (w_query, w_key, w_value, w_out, w_gate, w_up, w_down, gain_attn, gain_mlp)
+        last_parts = [v for i in range(num_layers) for v in (*done[i], *done[i, "down"])] + [gain_sums, y_out, grad]
+        *stacked, y_out, grad = pack(last_parts, [shape(m.shape, F32) for m in masters] + [shape(v.shape, BF) for v in (y_out, grad)])
+        return (jnp.swapaxes(y_out, 1, 2), jnp.swapaxes(grad, 1, 2), *stacked)
 
     in_specs = (shard_spec,) * 9 + (P(), P(), batch_spec, batch_spec)
     out_specs = (batch_spec, batch_spec) + (shard_spec,) * 9

time: 266 us -> 262 us (0.985)
  other arithmetic: 7.05 us -> 1.5 us
  Pallas kernels: 253 us -> 258 us
  local copies, waits for them, and re-layouts: 4.6 us -> 0.98 us
    another operation x6 -> x0, other arithmetic: 6.95 us -> none  [local_step(): stacked = tuple((jnp.stack(parts) for parts in zip(*grads)))]
    pallas_call x0 -> x1, Pallas kernels: none -> 5.51 us  [pack(): pl.pallas_call(pack_kernel, in_specs=[vmem] * len(parts), out_specs=[vmem...]
where the time goes in v3:
time: 262 us
  Pallas kernels  258 us (98%)
    pallas_call x3, Pallas kernels, fused(): pl.pallas_call(kernel, grid=(steps,), in_specs=in_specs, out_specs=out_sp...  172 us
    pallas_call x1, Pallas kernels, forward(): pl.pallas_call(kernel, grid=(3 * n,), in_specs=[pl.BlockSpec((1, DIM, SEQ...  81.3 us
    pallas_call x1, Pallas kernels, pack(): pl.pallas_call(pack_kernel, in_specs=[vmem] * len(parts), out_specs=[vmem...  5.51 us

profile of v3, /device:TPU:0, one launch (start us, length us, event | category | flops | bytes accessed | tf_op | source)
XLA Modules:
  0.0 261.7 jit_solution(1056268369693285867)
XLA Ops:
  0.6 81.3 %forward.1 = (bf16[8,256,576]{2,1,0:T(8,128)(2,1)}, bf16[8,256,960]{2,1,0:T(8,128)(2,1)}, bf16[8,3,384,128]{3,2,1,0:T(8,128)(2,1)}, bf16[8,3,384,256]{3,2,1,0:T(...) custom-call(bf16[4,576,256]{2,1,0:T(8,128)(2,1)} %bitcast.22, ...), custom_call_target="tpu_custom_call" | custom-call | flops 20000000000 | bytes 40000000 | tf_op jit(solution)/shard_map/forward/pallas_call | solution.py:516
  81.9 63.9 %layer_bwd.2 = (bf16[4,256,576]{2,1,0:T(8,128)(2,1)}, f32[4,1,576]{2,1,0:T(1,128)}, f32[4,72,960]{2,1,0:T(8,128)}, f32[4,72,960]{2,1,0:T(8,128)}, f32[4,72,576]{...) custom-call(bf16[8,256,576]{2,1,0:T(8,128)(2,1)} %get-tuple-element., ...), custom_call_target="tpu_custom_call" | custom-call | flops 30000001024 | bytes 20000000 | tf_op jit(solution)/shard_map/layer_bwd/pallas_call | solution.py:304
  145.8 0.0 copy-start.1
  145.8 0.0 copy-start
  145.8 74.2 %layer_bwd.3 = (bf16[4,576,256]{2,1,0:T(8,128)(2,1)}, f32[4,1,576]{2,1,0:T(1,128)}, f32[4,72,960]{2,1,0:T(8,128)}, f32[4,72,960]{2,1,0:T(8,128)}, f32[4,72,576]{...) custom-call(bf16[8,256,576]{2,1,0:T(8,128)(2,1)} %get-tuple-element., ...), custom_call_target="tpu_custom_call" | custom-call | flops 30000001024 | bytes 20000000 | tf_op jit(solution)/shard_map/layer_bwd/pallas_call | solution.py:304
  220.0 0.7 reduce_sum.36
  220.7 0.1 stack.15
  220.8 0.7 reduce_sum.37
  221.5 0.1 stack.16
  221.6 0.0 copy-done.1
  221.7 0.1 stack.17
  221.8 0.0 copy-done
  221.8 0.1 stack.18
  221.9 0.6 copy_bitcast_fusion
  222.6 33.6 %rs_tail.1 = (f32[72,1536]{1,0:T(8,128)}, f32[72,1536]{1,0:T(8,128)}, f32[72,960]{1,0:T(8,128)}, f32[72,576]{1,0:T(8,128)}, f32[8,128]{1,0:T(8,128)}) custom-call(f32[2,72,1536]{2,1,0:T(8,128)} %get-tuple-element.99.refs_0_, f32[2,72,1536]{2,1,0:T(8,128)} %get-tuple-element.100.refs_1_, f32[4,72,960]{2,1,0:T(8,128)} %get-tuple-element.101.refs_2_, ...), custom_call_target="tpu_custom_call" | custom-call | flops 1000000 | bytes 20000000 | tf_op jit(solution)/shard_map/rs_tail/pallas_call | solution.py:304
  256.2 5.5 %pack.1 = (f32[2,72,576]{2,1,0:T(8,128)}, f32[2,72,192]{2,1,0:T(8,128)}, f32[2,72,192]{2,1,0:T(8,128)}, f32[2,72,576]{2,1,0:T(8,128)}, f32[2,72,1536]{2,1,0:T(8,...) custom-call(f32[72,1536]{1,0:T(8,128)} %get-tuple-element.109.refs_0, ...), custom_call_target="tpu_custom_call" | custom-call | flops 1000000 | bytes 7000000 | tf_op jit(solution)/shard_map/pack/pallas_call | solution.py:736
  (4 shorter events, 0.1 us)
Async XLA Ops:
  145.8 75.8 %copy-start.1 = (f32[4,1,576]{2,1,0:T(1,128)S(1)}, f32[4,1,576]{2,1,0:T(1,128)}, u32[]{:S(2)}) copy-start(f32[4,1,576]{2,1,0:T(1,128)} %get-tuple-element.107) | copy-start | bytes 27652
  145.8 75.9 %copy-start = (f32[4,1,576]{2,1,0:T(1,128)S(1)}, f32[4,1,576]{2,1,0:T(1,128)}, u32[]{:S(2)}) copy-start(f32[4,1,576]{2,1,0:T(1,128)} %get-tuple-element.108) | copy-start | bytes 27652
